TPU v7x, 32 devices: a whole 2x2x4 slice. The times are simulated.
32 devices in a mesh: ta: 16 (over z, y, x), sa: 2 (over core).
Axes of the slice: x: 2, y: 2, z: 4, core: 2. Of those that a mesh axis runs over, the one named last changes fastest.
Arguments:
- rhs: float32 [1, 2, 40, 16, 2, 128], P(None, None, None, 'ta', 'sa'), may hold values from -6 to 6
- links: bfloat16 [4, 2, 40, 40, 16, 2, 128], P(None, None, None, None, 'ta', 'sa'), may hold values from -0.625 to 0.625
- clover: bfloat16 [2, 40, 40, 16, 2, 128], P(None, None, None, 'ta', 'sa'), may hold values from -1 to 7
- mr_steps: int32 [16, 2, 2], P('ta', 'sa'), may hold values from 2 to 3
Outputs:
- solution: float32 [1, 2, 40, 16, 2, 128], P(None, None, None, 'ta', 'sa')
- residual: float32 [1, 2, 40, 16, 2, 128], P(None, None, None, 'ta', 'sa')
All inputs are finite; a program needn't handle non-finite values.
Results may differ from a plain program's by a relative error of at most 0.0003.
Values sent between devices are 32-bit elements; how exact they have to be, the bound alone decides.
No kernel may reach another device: no remote copies, remote signals or barrier semaphores. Data moves between devices by JAX's collectives and lax.ppermute only.
A program may use at most 128 MiB of HBM per device.

v0:
```python
import functools

import jax
import jax.numpy as jnp
from jax import lax
from jax.experimental import pallas as pl
from jax.experimental.pallas import tpu as pltpu
from jax.sharding import PartitionSpec as P

LZ = 4
LY = 4
LX = 4
MR_MAX = 3
SWEEPS = 2
PLANE = LY * LX
UNIT = 4

F32 = jnp.float32
BF16 = jnp.bfloat16
VMEM = pl.BlockSpec(memory_space=pltpu.VMEM)
HBM = pl.BlockSpec(memory_space=pltpu.HBM)


def lanes(shape):
    return lax.broadcasted_iota(jnp.int32, shape, len(shape) - 1)


def sublanes(shape):
    return lax.broadcasted_iota(jnp.int32, shape, len(shape) - 2)


def low_half(shape):
    return lanes(shape) < shape[-1] // 2


def real_rows(shape):
    return sublanes(shape) % (2 * UNIT) < UNIT


def turn(x, amount):
    amount %= x.shape[-1]
    return pltpu.roll(x, amount, x.ndim - 1) if amount else x


def swap(x):
    return turn(x, x.shape[-1] // 2)


def tiles(x):
    return [x[k:k + 2 * UNIT] for k in range(0, x.shape[0], 2 * UNIT)]


def flip(x):
    return jnp.concatenate([pltpu.roll(t, UNIT, 0) for t in tiles(x)], 0)


def times_i(x):
    return jnp.where(real_rows(x.shape), -1.0, 1.0) * flip(x)


def chirality(shape):
    return jnp.where(low_half(shape), 1.0, -1.0).astype(F32)


def shifted(x, direction, sign, extra):
    place = lanes(x.shape) % (x.shape[-1] // 2)
    extent, stride = {1: (LZ, PLANE), 2: (LY, LX), 3: (LX, 1)}[direction]
    edge = place // stride % extent == (extent - 1 if sign > 0 else 0)
    inner = turn(x, extra - sign * stride)
    if direction == 1:
        return jnp.where(edge, 0.0, inner)
    return jnp.where(edge, turn(x, extra + sign * (extent - 1) * stride), inner)


def natural(x, y):
    low = low_half((2 * UNIT, x.shape[1]))
    real = real_rows(low.shape)
    pairs = list(zip(tiles(x), tiles(y)))
    units = [jnp.where(low, a, b) for a, b in pairs] + [jnp.where(low, b, a) for a, b in pairs]
    re, im = [], []
    for even, odd in zip(units[0::2], units[1::2]):
        re.append(jnp.where(real, even, pltpu.roll(odd, UNIT, 0)))
        im.append(jnp.where(real, pltpu.roll(even, UNIT, 0), odd))
    return jnp.concatenate(re, 0), jnp.concatenate(im, 0)


def unit_tiles(re, im):
    real = real_rows((2 * UNIT, re.shape[1]))
    out = []
    for a, b in zip(tiles(re), tiles(im)):
        out.append(jnp.where(real, a, pltpu.roll(b, UNIT, 0)))
        out.append(jnp.where(real, pltpu.roll(a, UNIT, 0), b))
    return out


def split(x):
    high = x.astype(BF16).astype(F32)
    return high, x - high


def gather_rows(parts):
    rows = sublanes(parts[0].shape)
    step = 1
    while len(parts) > 1:
        upper = (rows & step) != 0
        parts = [
            jnp.where(upper, odd, even) + pltpu.roll(jnp.where(upper, even, odd), step, 0)
            for even, odd in zip(parts[0::2], parts[1::2])
        ]
        step *= 2
    return parts[0]


def put_forward(x, y, ab_ref, slot):
    re, im = natural(x, y)
    for k, (r, i) in enumerate(zip(split(re), split(im))):
        ab_ref[slot, 0, k] = jnp.concatenate([r, -i], 0).astype(BF16)
        ab_ref[slot, 1, k] = jnp.concatenate([i, r], 0).astype(BF16)


def put_backward(x, rows_ref, spread_ref):
    dof, width = x.shape
    for k, part in enumerate(split(x * chirality(x.shape))):
        rows_ref[k] = part
        for row in range(dof):
            r, kind = UNIT * (row // (2 * UNIT)) + row % UNIT, row // UNIT % 2
            spread_ref[kind, k, r] = jnp.broadcast_to(rows_ref[k, row:row + 1, :], (16, width)).astype(BF16)


def forward_sums(terms, ab_ref, part_ref):
    entries, rows, width = terms[0][0].shape

    def body(group, carry):
        for own in range(2):
            r = 2 * group + own
            for kind in range(2):
                total = None
                for m_ref, slot in terms:
                    for t in range(0, rows, 16):
                        m = m_ref[r, pl.ds(t, 16), :].astype(F32)
                        for k in range(2):
                            product = m * ab_ref[slot, kind, k, pl.ds(t, 16), :].astype(F32)
                            total = product if total is None else total + product
                part_ref[kind, r] = total[:8] + total[8:]
        return carry

    lax.fori_loop(0, entries // 2, body, 0)
    out = []
    for t in range(0, entries, UNIT):
        parts = [part_ref[kind, t + k] for kind in range(2) for k in range(UNIT)]
        out.append(gather_rows(parts))
    return jnp.concatenate(out, 0)


def backward_sums(m_ref, spread_ref, back_ref):
    entries, rows, width = m_ref.shape
    starts = list(range(0, rows, 16))
    for pair in [starts[k:k + 2] for k in range(0, len(starts), 2)]:
        for t in pair:
            for kind in range(2):
                totals = [None] * (2 if len(pair) == 1 else 1)
                for r in range(entries):
                    m = m_ref[r, pl.ds(t, 16), :].astype(F32)
                    for k in range(2):
                        product = m * spread_ref[kind, k, r].astype(F32)
                        slot = k % len(totals)
                        totals[slot] = product if totals[slot] is None else totals[slot] + product
                back_ref[kind, pl.ds(t, 16), :] = totals[0] if len(totals) == 1 else totals[0] + totals[1]


def backward_halves(back_ref):
    dof = back_ref.shape[1] // 2
    re = back_ref[0, 0:dof, :] + back_ref[1, dof:2 * dof, :]
    im = back_ref[1, 0:dof, :] - back_ref[0, dof:2 * dof, :]
    units = unit_tiles(re, im)
    half = len(units) // 2
    low = low_half(units[0].shape)
    a = [jnp.where(low, p, q) for p, q in zip(units[:half], units[half:])]
    b = [jnp.where(low, q, p) for p, q in zip(units[:half], units[half:])]
    return jnp.concatenate(a, 0), jnp.concatenate(b, 0)


def block_operator(x, m_ref, ab_ref, rows_ref, spread_ref, back_ref, part_ref):
    half = x.shape[1] // 2
    put_forward(x, swap(x), ab_ref, 0)
    for direction in (1, 2, 3):
        put_forward(-shifted(x, direction, 1, 0), -shifted(x, direction, 1, half), ab_ref, direction)
    put_backward(x, rows_ref, spread_ref)

    def body(direction, carry):
        backward_sums(m_ref.at[direction], spread_ref, back_ref.at[direction])
        return carry

    lax.fori_loop(1, 4, body, 0)
    total = forward_sums([(m_ref.at[term], term) for term in range(4)], ab_ref, part_ref)
    backs = 0.0
    for direction in (1, 2, 3):
        a, b = backward_halves(back_ref.at[direction])
        backs = backs + shifted(a, direction, -1, 0) + shifted(b, direction, -1, half)
        if direction == 1:
            back_z = chirality(x.shape) * (a + swap(b))
    return total - chirality(x.shape) * backs, back_z


def backward_product(x, m_ref, rows_ref, spread_ref, back_ref):
    put_backward(x, rows_ref, spread_ref)
    backward_sums(m_ref, spread_ref, back_ref.at[0])
    a, b = backward_halves(back_ref.at[0])
    return chirality(x.shape) * (a + swap(b))


def total_of(x):
    return jnp.sum(jnp.sum(x, axis=0, keepdims=True), axis=1, keepdims=True)


def relax(residual, steps, m_ref, s_ref, e_ref, w_ref, work):
    s_ref[...] = residual
    e_ref[...] = jnp.zeros_like(residual)
    w_ref[...] = jnp.zeros_like(residual)

    def step(index, carry):
        s = s_ref[...]
        q, back_z = block_operator(s, m_ref, *work)
        s = s_ref[...]
        i_s = times_i(s)
        scale = total_of(q * q) + 1e-6
        live = index.astype(F32) < steps
        alpha_re = jnp.where(live, total_of(q * s) / scale, 0.0)
        alpha_im = jnp.where(live, -total_of(q * i_s) / scale, 0.0)
        e_ref[...] += alpha_re * s + alpha_im * i_s
        w_ref[...] += alpha_re * back_z + alpha_im * times_i(back_z)
        s_ref[...] = s - (alpha_re * q + alpha_im * times_i(q))
        return carry

    lax.fori_loop(0, MR_MAX, step, 0)


def send(half, e, w_ref, mt_ref, mz_ref, time_ref, rows_ref, spread_ref, back_ref):
    place = lanes(e.shape) % (e.shape[-1] // 2)
    mz_ref[...] = jnp.where(place // PLANE == 0, e, w_ref[...])

    @pl.when(half == 0)
    def _():
        mt_ref[...] = e

    @pl.when(half != 0)
    def _():
        mt_ref[...] = backward_product(e, time_ref, rows_ref, spread_ref, back_ref)


def half_mask(shape, half):
    return low_half(shape) == (half == 0)


def pack_matrix(raw_ref, half, own_ref, other_ref):
    dof = raw_ref.shape[1]
    entries = dof // 2
    mask = half_mask((dof, raw_ref.shape[-1]), half)

    def body(r, carry):
        for part in range(2):
            near = raw_ref[part, r + entries * half].astype(F32)
            far = raw_ref[part, r + entries * (1 - half)].astype(F32)
            own_ref[r, pl.ds(part * dof, dof), :] = jnp.where(mask, near, swap(far)).astype(BF16)
            other_ref[r, pl.ds(part * dof, dof), :] = jnp.where(mask, swap(near), far).astype(BF16)
        return carry

    lax.fori_loop(0, entries, body, 0, unroll=2)


def pack_field(ref, half):
    units = unit_tiles(ref[0], ref[1])
    count = len(units) // 2
    mask = half_mask(units[0].shape, half)
    first = jnp.concatenate(units[:count], 0)
    second = jnp.concatenate(units[count:], 0)
    own = jnp.where(half == 0, first, second)
    other = jnp.where(half == 0, second, first)
    return jnp.where(half_mask(own.shape, half), own, swap(other))


def unpack_fields(half, here, other, out_ref):
    first = natural(here, swap(here))
    second = natural(other, swap(other))
    for part in range(2):
        mask = half_mask(first[part].shape, half)
        out_ref[part] = jnp.where(mask, first[part], second[part])


def which(colour):
    return (colour + lax.axis_index("sa")) % 2


def fetch(pairs, sem):
    copies = [pltpu.make_async_copy(source, target, sem.at[k]) for k, (source, target) in enumerate(pairs)]
    for copy in copies:
        copy.start()
    return copies


def first_kernel(steps_in, rhs_in, links_in, clover_in, m_ref, time_ref, e_ref, s_ref, mt_ref, mz_ref, steps_ref,
                 m_other_ref, time_other_ref, r_ref, raw_ref, rhs_ref, count_ref, sem, w_ref, *work):
    half = which(0)
    pairs = [(rhs_in, rhs_ref), (steps_in, count_ref), (clover_in, raw_ref.at[0])]
    pairs += [(links_in.at[k % 4], raw_ref.at[k]) for k in (1, 2, 3, 4)]
    copies = fetch(pairs, sem)
    copies[0].wait()
    copies[1].wait()
    for k in range(2):
        steps_ref[k] = jnp.full(steps_ref.shape[1:], count_ref[0, 0, k].astype(F32))
    residual = pack_field(rhs_ref, half)
    r_ref[...] = pack_field(rhs_ref, 1 - half)
    for term in range(5):
        copies[2 + term].wait()
        if term == 4:
            pack_matrix(raw_ref.at[term], 1, time_ref, time_other_ref)
        else:
            pack_matrix(raw_ref.at[term], half, m_ref.at[term], m_other_ref.at[term])
    relax(residual, steps_ref[half, 0:1, 0:1], m_ref, s_ref, e_ref, w_ref, work)
    ab_ref, rows_ref, spread_ref, back_ref, part_ref = work
    send(half, e_ref[...], w_ref, mt_ref, mz_ref, time_ref, rows_ref, spread_ref, back_ref)


def local_part(half, e, base, time_ref, r_ref, ab_ref, rows_ref, spread_ref, back_ref, part_ref):
    @pl.when(half == 0)
    def _():
        r_ref[...] = base() + backward_product(e, time_ref, rows_ref, spread_ref, back_ref)

    @pl.when(half != 0)
    def _():
        put_forward(e, swap(e), ab_ref, 0)
        r_ref[...] = base() + forward_sums([(time_ref, 0)], ab_ref, part_ref)


def local_kernel(colour, e_ref, s_ref, time_ref, r_ref, *work):
    local_part(which(colour), e_ref[...], lambda: s_ref[...], time_ref, r_ref, *work)


def remote_part(half, r, mt, mz_up, mz_down, m_ref, time_ref, ab_ref, part_ref):
    depth = lanes(r.shape) % (r.shape[1] // 2) // PLANE
    reach = (LZ - 1) * PLANE
    top = depth == LZ - 1
    put_forward(jnp.where(top, turn(mz_up, reach), 0.0), jnp.where(top, turn(mz_up, reach + r.shape[1] // 2), 0.0), ab_ref, 0)
    ahead = jnp.where(half == 0, 0.0, mt)
    put_forward(ahead, swap(ahead), ab_ref, 1)
    total = r + jnp.where(depth == 0, turn(mz_down, -reach), 0.0) + jnp.where(half == 0, mt, 0.0)
    return total + forward_sums([(m_ref.at[1], 0), (time_ref, 1)], ab_ref, part_ref)


def sweep_kernel(colour, n_z, fresh, *refs):
    steps_ref, r_ref, mt_in, *refs = refs
    mz_in = refs[:n_z]
    m_ref, time_ref, *refs = refs[n_z:]
    if not fresh:
        sol_ref, *refs = refs
    e_ref, s_ref, new_ref, mt_ref, mz_ref, w_ref, *work = refs
    ab_ref, rows_ref, spread_ref, back_ref, part_ref = work
    half = which(colour)
    residual = remote_part(half, r_ref[...], mt_in[...], mz_in[0][...], mz_in[-1][...], m_ref, time_ref, ab_ref, part_ref)
    relax(residual, steps_ref[half, 0:1, 0:1], m_ref, s_ref, e_ref, w_ref, work)
    send(half, e_ref[...], w_ref, mt_ref, mz_ref, time_ref, rows_ref, spread_ref, back_ref)
    new_ref[...] = e_ref[...] if fresh else sol_ref[...] + e_ref[...]


def last_kernel(colour, n_z, *refs):
    r_ref, mt_in, *refs = refs
    mz_in = refs[:n_z]
    m_ref, time_ref, s_ref, x_here, x_other, sol_ref, res_ref, ab_ref, part_ref = refs[n_z:]
    half = which(colour)
    residual = remote_part(half, r_ref[...], mt_in[...], mz_in[0][...], mz_in[-1][...], m_ref, time_ref, ab_ref, part_ref)
    unpack_fields(half, residual, s_ref[...], res_ref)
    unpack_fields(half, x_here[...], x_other[...], sol_ref)


def shards(rhs, links, clover, mr_steps):
    dof = rhs.shape[2]
    width = rhs.shape[-1]
    rhs_local = rhs.reshape(2, dof, width)
    links_local = links.reshape(4, 2, dof, dof, width)
    clover_local = clover.reshape(2, dof, dof, width)
    n_t = lax.axis_size("ta")
    n_s = lax.axis_size("sa")
    n_z = 1 if n_s == 2 else 2

    vector = jax.ShapeDtypeStruct((dof, width), F32)
    matrix = jax.ShapeDtypeStruct((dof // 2, 2 * dof, width), BF16)
    matrices = jax.ShapeDtypeStruct((4,) + matrix.shape, BF16)
    counts = jax.ShapeDtypeStruct((2, 8, width), F32)
    pair = jax.ShapeDtypeStruct((2, dof, width), F32)
    field = pltpu.VMEM((dof, width), F32)
    ab = pltpu.VMEM((4, 2, 2, 2 * dof, width), BF16)
    part = pltpu.VMEM((2, dof // 2, 8, width), F32)
    work = [
        ab,
        pltpu.VMEM((2, dof, width), F32),
        pltpu.VMEM((2, 2, dof // 2, 16, width), BF16),
        pltpu.VMEM((4, 2, 2 * dof, width), F32),
        part,
    ]
    raw = pltpu.VMEM((5, 2, dof, dof, width), links.dtype)
    rhs_buffer = pltpu.VMEM((2, dof, width), F32)
    params = pltpu.CompilerParams(vmem_limit_bytes=20 << 20)

    def call(kernel, name, ins, outs, scratch):
        return pl.pallas_call(
            kernel,
            in_specs=ins,
            out_specs=[VMEM] * len(outs),
            out_shape=outs,
            scratch_shapes=scratch,
            compiler_params=params,
            name=name,
        )

    def exchange(colour, mt, mz):
        pairs = []
        for t in range(n_t):
            for s in range(n_s):
                goal = (t + 1) % n_t if (colour + s) % 2 else (t - 1) % n_t
                pairs.append((t * n_s + s, goal * n_s + s))
        mt_in = lax.ppermute(mt, ("ta", "sa"), pairs)
        mz_in = [lax.ppermute(mz, "sa", [(s, (s - 1) % n_s) for s in range(n_s)])]
        if n_z == 2:
            mz_in.append(lax.ppermute(mz, "sa", [(s, (s + 1) % n_s) for s in range(n_s)]))
        return mt_in, mz_in

    m0, time1, e, s0, mt, mz, steps, m1, time0, r = call(
        first_kernel, "first", [HBM] * 4,
        [matrices, matrix, vector, vector, vector, vector, counts, matrices, matrix, vector],
        [raw, rhs_buffer, pltpu.SMEM(mr_steps.shape, mr_steps.dtype), pltpu.SemaphoreType.DMA((7,)), field] + work,
    )(*[pltpu.with_memory_space_constraint(v, pltpu.HBM) for v in (mr_steps, rhs_local, links_local, clover_local)])

    def neighbours(colour, e, base):
        return call(functools.partial(local_kernel, colour), "local", [VMEM] * 3, [vector], work)(e, base, time0)[0]

    mt_in, mz_in = exchange(0, mt, mz)
    r = neighbours(0, e, r)
    blocks = [m0, m1]
    x = [e, None]
    kept = [s0, None]
    last = 2 * SWEEPS - 1
    for index in range(1, last + 1):
        colour = index % 2
        ins = [steps, r, mt_in, *mz_in, blocks[colour], time1]
        fresh = x[colour] is None
        if not fresh:
            ins.append(x[colour])
        e, kept[colour], x[colour], mt, mz = call(
            functools.partial(sweep_kernel, colour, n_z, fresh), "sweep", [VMEM] * len(ins), [vector] * 5, [field] + work
        )(*ins)
        mt_in, mz_in = exchange(colour, mt, mz)
        r = neighbours(colour, e, kept[1 - colour])
    colour = (last + 1) % 2
    ins = [r, mt_in, *mz_in, blocks[colour], time1, kept[1 - colour], x[colour], x[1 - colour]]
    sol, res = call(functools.partial(last_kernel, colour, n_z), "last", [VMEM] * len(ins), [pair, pair], [ab, part])(*ins)
    return sol.reshape(rhs.shape), res.reshape(rhs.shape)


def solution(mesh):
    field = P(None, None, None, "ta", "sa", None)
    placed = (field, P(None, None, None, None, "ta", "sa", None), field, P("ta", "sa", None))
    return jax.shard_map(shards, mesh=mesh, in_specs=placed, out_specs=(field, field), check_vma=False)
```

profile of v0, /device:TPU:0, one launch (start us, length us, event | category | flops | bytes accessed | tf_op | source)
XLA Modules:
  0.0 50.3 jit_solution(2852687219810910754)
XLA Ops:
  0.6 9.3 %first.1 = (bf16[4,20,80,128]{3,2,1,0:T(8,128)(2,1)S(1)}, bf16[20,80,128]{2,1,0:T(8,128)(2,1)S(1)}, f32[40,128]{1,0:T(8,128)S(1)}, f32[40,128]{1,0:T(8,128)S(1)}...) custom-call(s32[1,1,2]{2,1,0:T(1,128)} %steps_in.1, ...), custom_call_target="tpu_custom_call" | custom-call | tf_op jit(solution)/shard_map/first/pallas_call | solution.py:427
  9.9 7.0 %collective-permute-start = (f32[40,128]{1,0:T(8,128)S(1)}, f32[40,128]{1,0:T(8,128)S(1)}, u32[]{:S(2)}, u32[]{:S(2)}) collective-permute-start(f32[40,128]{1,0:T(8,128)S(1)} %get-tuple-element.33), channel_id=1, source_target_pairs={{0,30},{1,3},{2,0},{3,5},{4,2},{5,7},{6,4},{7,9},{8,6},{9,11},{10,... | collective-permute-start | bytes 61448 | tf_op jit(solution)/shard_map/ppermute | solution.py:421
  16.9 0.0 collective-permute-start.1
  16.9 0.2 local.4.refs_1_
  17.1 1.3 %collective-permute-done.refs_2_ = f32[40,128]{1,0:T(8,128)S(1)} collective-permute-done((f32[40,128]{1,0:T(8,128)S(1)}, f32[40,128]{1,0:T(8,128)S(1)}, u32[]{:S(2)}, u32[]{:S(2)}) %collective-permute-start) | collective-permute-done | bytes 20512 | tf_op jit(solution)/shard_map/ppermute | solution.py:421
  18.4 0.0 collective-permute-done.1.refs_3_
  18.4 4.0 %sweep.3 = (f32[40,128]{1,0:T(8,128)S(1)}, f32[40,128]{1,0:T(8,128)S(1)}, f32[40,128]{1,0:T(8,128)S(1)}, f32[40,128]{1,0:T(8,128)S(1)}, f32[40,128]{1,0:T(8,128)S(1)}) custom-call(f32[2,8,128]{2,1,0:T(8,128)S(1)} %get-tuple-element.29.refs_0_, f32[40,128]{1,0:T(8,128)S(1)} %local.4.refs_1_, f32[40,128]{1,0:T(8,128)S(1)} %collective-permute-done.refs_2_, ...), custom_call_target="tpu_custom_call" | custom-call | tf_op jit(solution)/shard_map/sweep/pallas_call | solution.py:448
  22.4 0.1 collective-permute-start.2
  22.5 0.7 %collective-permute-start.3 = (f32[40,128]{1,0:T(8,128)S(1)}, f32[40,128]{1,0:T(8,128)S(1)}, u32[]{:S(2)}, u32[]{:S(2)}) collective-permute-start(f32[40,128]{1,0:T(8,128)S(1)} %get-tuple-element.40), channel_id=1, source_target_pairs={{0,1},{1,0},{2,3},{3,2},{4,5},{5,4},{6,7},{7,6},{8,9},{9,8},{10,11... | collective-permute-start | bytes 61448 | tf_op jit(solution)/shard_map/ppermute | solution.py:422
  23.2 0.3 local.5.refs_1_
  23.5 6.6 %collective-permute-done.2.refs_2_ = f32[40,128]{1,0:T(8,128)S(1)} collective-permute-done((f32[40,128]{1,0:T(8,128)S(1)}, f32[40,128]{1,0:T(8,128)S(1)}, u32[]{:S(2)}, u32[]{:S(2)}) %collective-permute-start.2) | collective-permute-done | bytes 20512 | tf_op jit(solution)/shard_map/ppermute | solution.py:421
  30.1 0.0 collective-permute-done.3.refs_3_
  30.1 3.8 %sweep.4 = (f32[40,128]{1,0:T(8,128)S(1)}, f32[40,128]{1,0:T(8,128)S(1)}, f32[40,128]{1,0:T(8,128)S(1)}, f32[40,128]{1,0:T(8,128)S(1)}, f32[40,128]{1,0:T(8,128)S(1)}) custom-call(f32[2,8,128]{2,1,0:T(8,128)S(1)} %get-tuple-element.29.refs_0_, f32[40,128]{1,0:T(8,128)S(1)} %local.5.refs_1_, f32[40,128]{1,0:T(8,128)S(1)} %collective-permute-done.2.refs_2_, ...), custom_call_target="tpu_custom_call" | custom-call | tf_op jit(solution)/shard_map/sweep/pallas_call | solution.py:448
  34.0 2.1 %collective-permute-start.4 = (f32[40,128]{1,0:T(8,128)S(1)}, f32[40,128]{1,0:T(8,128)S(1)}, u32[]{:S(2)}, u32[]{:S(2)}) collective-permute-start(f32[40,128]{1,0:T(8,128)S(1)} %get-tuple-element.44), channel_id=1, source_target_pairs={{0,30},{1,3},{2,0},{3,5},{4,2},{5,7},{6,4},{7,9},{8,6},{9,11},{10,... | collective-permute-start | bytes 61448 | tf_op jit(solution)/shard_map/ppermute | solution.py:421
  36.0 0.0 collective-permute-start.5
  36.0 0.2 local.6.refs_1_
  36.2 1.6 %collective-permute-done.4.refs_2_ = f32[40,128]{1,0:T(8,128)S(1)} collective-permute-done((f32[40,128]{1,0:T(8,128)S(1)}, f32[40,128]{1,0:T(8,128)S(1)}, u32[]{:S(2)}, u32[]{:S(2)}) %collective-permute-start.4) | collective-permute-done | bytes 20512 | tf_op jit(solution)/shard_map/ppermute | solution.py:421
  37.8 0.0 collective-permute-done.5.refs_3_
  37.8 4.0 %sweep.5 = (f32[40,128]{1,0:T(8,128)S(1)}, f32[40,128]{1,0:T(8,128)S(1)}, f32[40,128]{1,0:T(8,128)S(1)}, f32[40,128]{1,0:T(8,128)S(1)}, f32[40,128]{1,0:T(8,128)S(1)}) custom-call(f32[2,8,128]{2,1,0:T(8,128)S(1)} %get-tuple-element.29.refs_0_, f32[40,128]{1,0:T(8,128)S(1)} %local.6.refs_1_, f32[40,128]{1,0:T(8,128)S(1)} %collective-permute-done.4.refs_2_, ...), custom_call_target="tpu_custom_call" | custom-call | tf_op jit(solution)/shard_map/sweep/pallas_call | solution.py:448
  41.8 0.1 collective-permute-start.6
  41.9 0.1 collective-permute-start.7
  41.9 0.3 local.7.refs_0_
  42.3 6.9 %collective-permute-done.6.refs_1_ = f32[40,128]{1,0:T(8,128)S(1)} collective-permute-done((f32[40,128]{1,0:T(8,128)S(1)}, f32[40,128]{1,0:T(8,128)S(1)}, u32[]{:S(2)}, u32[]{:S(2)}) %collective-permute-start.6) | collective-permute-done | bytes 20512 | tf_op jit(solution)/shard_map/ppermute | solution.py:421
  49.2 0.0 collective-permute-done.7.refs_2_
  49.2 1.0 %last.1 = (f32[2,40,128]{2,1,0:T(8,128)}, f32[2,40,128]{2,1,0:T(8,128)}) custom-call(f32[40,128]{1,0:T(8,128)S(1)} %local.7.refs_0_, f32[40,128]{1,0:T(8,128)S(1)} %collective-permute-done.6.refs_1_, f32[40,128]{1,0:T(8,128)S(1)} %collective-permute-done.7.refs_2_, bf16[4,20,80,128]{3,2,1,0:T(8,128)(2,1)S(1)} %get-tuple-element.41.refs_4_.refs_3_, ...), custom_call_target="tpu_custom_call" | custom-call | tf_op jit(solution)/shard_map/last/pallas_call | solution.py:455
Async XLA Ops:
  9.9 8.5 %collective-permute-start = (f32[40,128]{1,0:T(8,128)S(1)}, f32[40,128]{1,0:T(8,128)S(1)}, u32[]{:S(2)}, u32[]{:S(2)}) collective-permute-start(f32[40,128]{1,0:T(8,128)S(1)} %get-tuple-element.33), channel_id=1, source_target_pairs={{0,30},{1,3},{2,0},{3,5},{4,2},{5,7},{6,4},{7,9},{8,6},{9,11},{10,... | collective-permute-start | bytes 61448 | tf_op jit(solution)/shard_map/ppermute | solution.py:421
  16.9 1.5 %collective-permute-start.1 = (f32[40,128]{1,0:T(8,128)S(1)}, f32[40,128]{1,0:T(8,128)S(1)}, u32[]{:S(2)}, u32[]{:S(2)}) collective-permute-start(f32[40,128]{1,0:T(8,128)S(1)} %get-tuple-element.34), channel_id=1, source_target_pairs={{0,1},{1,0},{2,3},{3,2},{4,5},{5,4},{6,7},{7,6},{8,9},{9,8},{10,11... | collective-permute-start | bytes 61448 | tf_op jit(solution)/shard_map/ppermute | solution.py:422
  22.4 7.7 %collective-permute-start.2 = (f32[40,128]{1,0:T(8,128)S(1)}, f32[40,128]{1,0:T(8,128)S(1)}, u32[]{:S(2)}, u32[]{:S(2)}) collective-permute-start(f32[40,128]{1,0:T(8,128)S(1)} %get-tuple-element.39), channel_id=1, source_target_pairs={{0,2},{1,31},{2,4},{3,1},{4,6},{5,3},{6,8},{7,5},{8,10},{9,7},{10,... | collective-permute-start | bytes 61448 | tf_op jit(solution)/shard_map/ppermute | solution.py:421
  22.5 7.6 %collective-permute-start.3 = (f32[40,128]{1,0:T(8,128)S(1)}, f32[40,128]{1,0:T(8,128)S(1)}, u32[]{:S(2)}, u32[]{:S(2)}) collective-permute-start(f32[40,128]{1,0:T(8,128)S(1)} %get-tuple-element.40), channel_id=1, source_target_pairs={{0,1},{1,0},{2,3},{3,2},{4,5},{5,4},{6,7},{7,6},{8,9},{9,8},{10,11... | collective-permute-start | bytes 61448 | tf_op jit(solution)/shard_map/ppermute | solution.py:422
  34.0 3.8 %collective-permute-start.4 = (f32[40,128]{1,0:T(8,128)S(1)}, f32[40,128]{1,0:T(8,128)S(1)}, u32[]{:S(2)}, u32[]{:S(2)}) collective-permute-start(f32[40,128]{1,0:T(8,128)S(1)} %get-tuple-element.44), channel_id=1, source_target_pairs={{0,30},{1,3},{2,0},{3,5},{4,2},{5,7},{6,4},{7,9},{8,6},{9,11},{10,... | collective-permute-start | bytes 61448 | tf_op jit(solution)/shard_map/ppermute | solution.py:421
  36.0 1.8 %collective-permute-start.5 = (f32[40,128]{1,0:T(8,128)S(1)}, f32[40,128]{1,0:T(8,128)S(1)}, u32[]{:S(2)}, u32[]{:S(2)}) collective-permute-start(f32[40,128]{1,0:T(8,128)S(1)} %get-tuple-element.45), channel_id=1, source_target_pairs={{0,1},{1,0},{2,3},{3,2},{4,5},{5,4},{6,7},{7,6},{8,9},{9,8},{10,11... | collective-permute-start | bytes 61448 | tf_op jit(solution)/shard_map/ppermute | solution.py:422
  41.8 7.4 %collective-permute-start.6 = (f32[40,128]{1,0:T(8,128)S(1)}, f32[40,128]{1,0:T(8,128)S(1)}, u32[]{:S(2)}, u32[]{:S(2)}) collective-permute-start(f32[40,128]{1,0:T(8,128)S(1)} %get-tuple-element.49), channel_id=1, source_target_pairs={{0,2},{1,31},{2,4},{3,1},{4,6},{5,3},{6,8},{7,5},{8,10},{9,7},{10,... | collective-permute-start | bytes 61448 | tf_op jit(solution)/shard_map/ppermute | solution.py:421
  41.9 7.4 %collective-permute-start.7 = (f32[40,128]{1,0:T(8,128)S(1)}, f32[40,128]{1,0:T(8,128)S(1)}, u32[]{:S(2)}, u32[]{:S(2)}) collective-permute-start(f32[40,128]{1,0:T(8,128)S(1)} %get-tuple-element.50), channel_id=1, source_target_pairs={{0,1},{1,0},{2,3},{3,2},{4,5},{5,4},{6,7},{7,6},{8,9},{9,8},{10,11... | collective-permute-start | bytes 61448 | tf_op jit(solution)/shard_map/ppermute | solution.py:422
where the time goes:
time: 50.4 us; the launch traced here: 50.3 us
  Pallas kernels  23.2 us (46%)
  waiting for transfers between devices  16.4 us (33%)
  starting transfers between devices  9.98 us (20%)
  between operations  0.69 us (1%)
    ppermute x4, waiting for transfers between devices, exchange(): mt_in = lax.ppermute(mt, ('ta', 'sa'), pairs)  16.4 us
    pallas_call x3, Pallas kernels, shards(): call(functools.partial(sweep_kernel, colour, n_z, fresh), 'sweep', [VMEM]...  11.8 us
    pallas_call x1, Pallas kernels, shards(): call(first_kernel, 'first', [HBM] * 4, [matrices, matrix, vector, vector,...  9.27 us
    ppermute x4, starting transfers between devices, exchange(): mt_in = lax.ppermute(mt, ('ta', 'sa'), pairs)  9.2 us
    pallas_call x1, Pallas kernels, shards(): call(functools.partial(last_kernel, colour, n_z), 'last', [VMEM] * len(in...  1.05 us
    pallas_call x4, Pallas kernels, neighbours(): call(functools.partial(local_kernel, colour), 'local', [VMEM] * 3, [vecto...  1.02 us
  transfers between devices with their start and end apart: 8, of which 4 were waited for; matrix products, arithmetic and copies ran while one was open for 0% of the time, Pallas kernels for 2%

commit v1 on v0

--- a/solution.py
+++ b/solution.py
@@ -6,6 +6,7 @@
 from jax.experimental import pallas as pl
 from jax.experimental.pallas import tpu as pltpu
 from jax.sharding import PartitionSpec as P
+
 
 LZ = 4
 LY = 4
@@ -14,6 +15,7 @@
 SWEEPS = 2
 PLANE = LY * LX
 UNIT = 4
+PIECES = 2
 
 F32 = jnp.float32
 BF16 = jnp.bfloat16
@@ -127,8 +129,8 @@
             spread_ref[kind, k, r] = jnp.broadcast_to(rows_ref[k, row:row + 1, :], (16, width)).astype(BF16)
 
 
-def forward_sums(terms, ab_ref, part_ref):
-    entries, rows, width = terms[0][0].shape
+def forward_sums(terms, ab_ref, part_ref, unroll=1):
+    entries, rows, _ = terms[0][0].shape
 
     def body(group, carry):
         for own in range(2):
@@ -144,7 +146,7 @@
                 part_ref[kind, r] = total[:8] + total[8:]
         return carry
 
-    lax.fori_loop(0, entries // 2, body, 0)
+    lax.fori_loop(0, entries // 2, body, 0, unroll=unroll)
     out = []
     for t in range(0, entries, UNIT):
         parts = [part_ref[kind, t + k] for kind in range(2) for k in range(UNIT)]
@@ -153,7 +155,7 @@
 
 
 def backward_sums(m_ref, spread_ref, back_ref):
-    entries, rows, width = m_ref.shape
+    entries, rows, _ = m_ref.shape
     starts = list(range(0, rows, 16))
     for pair in [starts[k:k + 2] for k in range(0, len(starts), 2)]:
         for t in pair:
@@ -180,19 +182,16 @@
     return jnp.concatenate(a, 0), jnp.concatenate(b, 0)
 
 
-def block_operator(x, m_ref, ab_ref, rows_ref, spread_ref, back_ref, part_ref):
+def block_operator(x, unroll, m_ref, ab_ref, rows_ref, spread_ref, back_ref, part_ref):
     half = x.shape[1] // 2
     put_forward(x, swap(x), ab_ref, 0)
     for direction in (1, 2, 3):
         put_forward(-shifted(x, direction, 1, 0), -shifted(x, direction, 1, half), ab_ref, direction)
     put_backward(x, rows_ref, spread_ref)
 
-    def body(direction, carry):
+    for direction in (1, 2, 3):
         backward_sums(m_ref.at[direction], spread_ref, back_ref.at[direction])
-        return carry
-
-    lax.fori_loop(1, 4, body, 0)
-    total = forward_sums([(m_ref.at[term], term) for term in range(4)], ab_ref, part_ref)
+    total = forward_sums([(m_ref.at[term], term) for term in range(4)], ab_ref, part_ref, unroll)
     backs = 0.0
     for direction in (1, 2, 3):
         a, b = backward_halves(back_ref.at[direction])
@@ -210,29 +209,41 @@
 
 
 def total_of(x):
-    return jnp.sum(jnp.sum(x, axis=0, keepdims=True), axis=1, keepdims=True)
-
-
-def relax(residual, steps, m_ref, s_ref, e_ref, w_ref, work):
-    s_ref[...] = residual
-    e_ref[...] = jnp.zeros_like(residual)
-    w_ref[...] = jnp.zeros_like(residual)
+    parts = tiles(x)
+    total = parts[0]
+    for part in parts[1:]:
+        total = total + part
+    for amount in (4, 2, 1):
+        total = total + pltpu.roll(total, amount, 0)
+    return jnp.broadcast_to(jnp.sum(total, axis=1, keepdims=True), total.shape)
+
+
+def scaled(alpha, x):
+    return jnp.concatenate([alpha * tile for tile in tiles(x)], 0)
+
+
+def relax(residual, steps, m_ref, s_ref, e_ref, w_ref, work, mine=None):
+    @pl.when(True if mine is None else mine)
+    def _():
+        s_ref[...] = residual
+        e_ref[...] = jnp.zeros_like(residual)
+        w_ref[...] = jnp.zeros_like(residual)
 
     def step(index, carry):
         s = s_ref[...]
-        q, back_z = block_operator(s, m_ref, *work)
+        q, back_z = block_operator(s, s.shape[0] // (4 if mine is None else 8), m_ref, *work)
         s = s_ref[...]
         i_s = times_i(s)
         scale = total_of(q * q) + 1e-6
         live = index.astype(F32) < steps
         alpha_re = jnp.where(live, total_of(q * s) / scale, 0.0)
         alpha_im = jnp.where(live, -total_of(q * i_s) / scale, 0.0)
-        e_ref[...] += alpha_re * s + alpha_im * i_s
-        w_ref[...] += alpha_re * back_z + alpha_im * times_i(back_z)
-        s_ref[...] = s - (alpha_re * q + alpha_im * times_i(q))
+        e_ref[...] += scaled(alpha_re, s) + scaled(alpha_im, i_s)
+        w_ref[...] += scaled(alpha_re, back_z) + scaled(alpha_im, times_i(back_z))
+        s_ref[...] = s - (scaled(alpha_re, q) + scaled(alpha_im, times_i(q)))
         return carry
 
-    lax.fori_loop(0, MR_MAX, step, 0)
+    lax.fori_loop(0, MR_MAX if mine is None else jnp.where(mine, MR_MAX, 0), step, 0)
 
 
 def send(half, e, w_ref, mt_ref, mz_ref, time_ref, rows_ref, spread_ref, back_ref):
@@ -265,7 +276,7 @@
             other_ref[r, pl.ds(part * dof, dof), :] = jnp.where(mask, swap(near), far).astype(BF16)
         return carry
 
-    lax.fori_loop(0, entries, body, 0, unroll=2)
+    lax.fori_loop(0, entries, body, 0, unroll=10)
 
 
 def pack_field(ref, half):
@@ -298,27 +309,57 @@
     return copies
 
 
-def first_kernel(steps_in, rhs_in, links_in, clover_in, m_ref, time_ref, e_ref, s_ref, mt_ref, mz_ref, steps_ref,
-                 m_other_ref, time_other_ref, r_ref, raw_ref, rhs_ref, count_ref, sem, w_ref, *work):
+def first_turn(late):
+    early = lax.axis_index("ta") % 2 == which(0)
+    return jnp.logical_not(early) if late else early
+
+
+def pack_kernel(late, *refs):
+    steps_in, rhs_in, links_in, clover_in, *refs = refs
+    if late:
+        refs = refs[7:]
+    (m_ref, time_ref, m_other_ref, time_other_ref, own_ref, other_ref, steps_ref,
+     raw_ref, rhs_ref, count_ref, sem) = refs
     half = which(0)
-    pairs = [(rhs_in, rhs_ref), (steps_in, count_ref), (clover_in, raw_ref.at[0])]
-    pairs += [(links_in.at[k % 4], raw_ref.at[k]) for k in (1, 2, 3, 4)]
-    copies = fetch(pairs, sem)
-    copies[0].wait()
-    copies[1].wait()
-    for k in range(2):
-        steps_ref[k] = jnp.full(steps_ref.shape[1:], count_ref[0, 0, k].astype(F32))
-    residual = pack_field(rhs_ref, half)
-    r_ref[...] = pack_field(rhs_ref, 1 - half)
-    for term in range(5):
-        copies[2 + term].wait()
-        if term == 4:
-            pack_matrix(raw_ref.at[term], 1, time_ref, time_other_ref)
-        else:
-            pack_matrix(raw_ref.at[term], half, m_ref.at[term], m_other_ref.at[term])
-    relax(residual, steps_ref[half, 0:1, 0:1], m_ref, s_ref, e_ref, w_ref, work)
-    ab_ref, rows_ref, spread_ref, back_ref, part_ref = work
-    send(half, e_ref[...], w_ref, mt_ref, mz_ref, time_ref, rows_ref, spread_ref, back_ref)
+
+    @pl.when(first_turn(late))
+    def _():
+        dof = rhs_ref.shape[1]
+        pieces = []
+        for term in range(5):
+            source = clover_in if term == 0 else links_in.at[term % 4]
+            for part in range(2):
+                for row in range(0, dof, dof // PIECES):
+                    rows = pl.ds(row, dof // PIECES)
+                    pieces.append((source.at[part, rows], raw_ref.at[term, part, rows]))
+        copies = fetch(pieces + [(rhs_in, rhs_ref), (steps_in, count_ref)], sem)
+        for term in range(5):
+            for copy in copies[2 * PIECES * term:2 * PIECES * (term + 1)]:
+                copy.wait()
+            if term == 4:
+                pack_matrix(raw_ref.at[term], 1, time_ref, time_other_ref)
+            else:
+                pack_matrix(raw_ref.at[term], half, m_ref.at[term], m_other_ref.at[term])
+        copies[-2].wait()
+        copies[-1].wait()
+        for k in range(2):
+            steps_ref[k] = jnp.full(steps_ref.shape[1:], count_ref[0, 0, k].astype(F32))
+        own_ref[...] = pack_field(rhs_ref, half)
+        other_ref[...] = pack_field(rhs_ref, 1 - half)
+
+
+def first_kernel(late, steps_ref, r_ref, m_ref, time_ref, *refs):
+    if late:
+        refs = refs[3:]
+    e_ref, s_ref, mz_ref, mt_ref, w_ref, *work = refs
+    _, rows_ref, spread_ref, back_ref, _ = work
+    half = which(0)
+    mine = first_turn(late)
+    relax(r_ref[...], steps_ref[half], m_ref, s_ref, e_ref, w_ref, work, mine)
+
+    @pl.when(mine)
+    def _():
+        send(half, e_ref[...], w_ref, mt_ref, mz_ref, time_ref, rows_ref, spread_ref, back_ref)
 
 
 def local_part(half, e, base, time_ref, r_ref, ab_ref, rows_ref, spread_ref, back_ref, part_ref):
@@ -332,8 +373,14 @@
         r_ref[...] = base() + forward_sums([(time_ref, 0)], ab_ref, part_ref)
 
 
-def local_kernel(colour, e_ref, s_ref, time_ref, r_ref, *work):
-    local_part(which(colour), e_ref[...], lambda: s_ref[...], time_ref, r_ref, *work)
+def local_kernel(colour, e_ref, s_ref, time_ref, *refs):
+    half = which(colour)
+    if len(refs) > 6:
+        x_here, x_other, r_ref, sol_ref, *work = refs
+        unpack_fields(half, x_here[...], x_other[...], sol_ref)
+    else:
+        r_ref, *work = refs
+    local_part(half, e_ref[...], lambda: s_ref[...], time_ref, r_ref, *work)
 
 
 def remote_part(half, r, mt, mz_up, mz_down, m_ref, time_ref, ab_ref, part_ref):
@@ -347,29 +394,35 @@
     return total + forward_sums([(m_ref.at[1], 0), (time_ref, 1)], ab_ref, part_ref)
 
 
-def sweep_kernel(colour, n_z, fresh, *refs):
-    steps_ref, r_ref, mt_in, *refs = refs
-    mz_in = refs[:n_z]
-    m_ref, time_ref, *refs = refs[n_z:]
+def sweep_kernel(colour, n_t_in, n_z, fresh, *refs):
+    steps_ref, r_ref, *refs = refs
+    mt, mz_up, mz_down, refs = arrivals(refs, n_t_in, n_z)
+    m_ref, time_ref, *refs = refs
     if not fresh:
         sol_ref, *refs = refs
-    e_ref, s_ref, new_ref, mt_ref, mz_ref, w_ref, *work = refs
+    e_ref, s_ref, new_ref, mz_ref, mt_ref, w_ref, *work = refs
     ab_ref, rows_ref, spread_ref, back_ref, part_ref = work
     half = which(colour)
-    residual = remote_part(half, r_ref[...], mt_in[...], mz_in[0][...], mz_in[-1][...], m_ref, time_ref, ab_ref, part_ref)
-    relax(residual, steps_ref[half, 0:1, 0:1], m_ref, s_ref, e_ref, w_ref, work)
+    residual = remote_part(half, r_ref[...], mt, mz_up, mz_down, m_ref, time_ref, ab_ref, part_ref)
+    relax(residual, steps_ref[half], m_ref, s_ref, e_ref, w_ref, work)
     send(half, e_ref[...], w_ref, mt_ref, mz_ref, time_ref, rows_ref, spread_ref, back_ref)
     new_ref[...] = e_ref[...] if fresh else sol_ref[...] + e_ref[...]
 
 
-def last_kernel(colour, n_z, *refs):
-    r_ref, mt_in, *refs = refs
-    mz_in = refs[:n_z]
-    m_ref, time_ref, s_ref, x_here, x_other, sol_ref, res_ref, ab_ref, part_ref = refs[n_z:]
+def arrivals(refs, n_t_in, n_z):
+    mt = refs[0][...]
+    if n_t_in == 2:
+        mt = jnp.where(first_turn(False), refs[1][...], mt)
+    up, down = refs[n_t_in], refs[n_t_in + n_z - 1]
+    return mt, up[...], down[...], refs[n_t_in + n_z:]
+
+
+def last_kernel(colour, n_z, r_ref, *refs):
+    mt, mz_up, mz_down, refs = arrivals(refs, 1, n_z)
+    m_ref, time_ref, s_ref, res_ref, ab_ref, part_ref = refs
     half = which(colour)
-    residual = remote_part(half, r_ref[...], mt_in[...], mz_in[0][...], mz_in[-1][...], m_ref, time_ref, ab_ref, part_ref)
+    residual = remote_part(half, r_ref[...], mt, mz_up, mz_down, m_ref, time_ref, ab_ref, part_ref)
     unpack_fields(half, residual, s_ref[...], res_ref)
-    unpack_fields(half, x_here[...], x_other[...], sol_ref)
 
 
 def shards(rhs, links, clover, mr_steps):
@@ -401,59 +454,79 @@
     rhs_buffer = pltpu.VMEM((2, dof, width), F32)
     params = pltpu.CompilerParams(vmem_limit_bytes=20 << 20)
 
-    def call(kernel, name, ins, outs, scratch):
+    def call(kernel, ins, outs, scratch, specs=None, aliases={}):
         return pl.pallas_call(
             kernel,
-            in_specs=ins,
+            in_specs=specs or [VMEM] * len(ins),
             out_specs=[VMEM] * len(outs),
             out_shape=outs,
             scratch_shapes=scratch,
             compiler_params=params,
-            name=name,
-        )
-
-    def exchange(colour, mt, mz):
+            input_output_aliases=aliases,
+        )(*ins)
+
+    def time_pairs(colour, late=None):
         pairs = []
         for t in range(n_t):
             for s in range(n_s):
-                goal = (t + 1) % n_t if (colour + s) % 2 else (t - 1) % n_t
-                pairs.append((t * n_s + s, goal * n_s + s))
-        mt_in = lax.ppermute(mt, ("ta", "sa"), pairs)
-        mz_in = [lax.ppermute(mz, "sa", [(s, (s - 1) % n_s) for s in range(n_s)])]
+                half = (colour + s) % 2
+                if late is None or (t % 2 != half) == late:
+                    goal = (t + 1) % n_t if half else (t - 1) % n_t
+                    pairs.append((t * n_s + s, goal * n_s + s))
+                elif late and n_s % 2 == 0 and n_t % 2 == 0:
+                    pairs.append((t * n_s + s, t * n_s + (s + 1) % n_s))
+        return pairs
+
+    def along_time(mt, colour, late=None):
+        return lax.ppermute(mt, ("ta", "sa"), time_pairs(colour, late))
+
+    def along_z(mz):
+        got = [lax.ppermute(mz, "sa", [(s, (s - 1) % n_s) for s in range(n_s)])]
         if n_z == 2:
-            mz_in.append(lax.ppermute(mz, "sa", [(s, (s + 1) % n_s) for s in range(n_s)]))
-        return mt_in, mz_in
-
-    m0, time1, e, s0, mt, mz, steps, m1, time0, r = call(
-        first_kernel, "first", [HBM] * 4,
-        [matrices, matrix, vector, vector, vector, vector, counts, matrices, matrix, vector],
-        [raw, rhs_buffer, pltpu.SMEM(mr_steps.shape, mr_steps.dtype), pltpu.SemaphoreType.DMA((7,)), field] + work,
-    )(*[pltpu.with_memory_space_constraint(v, pltpu.HBM) for v in (mr_steps, rhs_local, links_local, clover_local)])
-
-    def neighbours(colour, e, base):
-        return call(functools.partial(local_kernel, colour), "local", [VMEM] * 3, [vector], work)(e, base, time0)[0]
-
-    mt_in, mz_in = exchange(0, mt, mz)
-    r = neighbours(0, e, r)
+            got.append(lax.ppermute(mz, "sa", [(s, (s + 1) % n_s) for s in range(n_s)]))
+        return got
+
+    args = [pltpu.with_memory_space_constraint(v, pltpu.HBM) for v in (mr_steps, rhs_local, links_local, clover_local)]
+    outs = [matrices, matrix, matrices, matrix, vector, vector, counts]
+    scratch = [raw, rhs_buffer, pltpu.SMEM(mr_steps.shape, mr_steps.dtype), pltpu.SemaphoreType.DMA((10 * PIECES + 2,))]
+    packed = call(functools.partial(pack_kernel, False), args, outs, scratch, [HBM] * 4)
+    m0, time1, m1, time0, own, r, steps = packed
+    early = call(functools.partial(first_kernel, False), [steps, own, m0, time1], [vector] * 4, [field] + work)
+    mt_a = along_time(early[-1], 0, False)
+    m0, time1, m1, time0, own, r, steps = call(
+        functools.partial(pack_kernel, True), [*args, *packed], outs, scratch,
+        [HBM] * 4 + [VMEM] * 7, {4 + k: k for k in range(7)},
+    )
+    e, s0, mz, mt = call(
+        functools.partial(first_kernel, True), [steps, own, m0, time1, *early[:-1]], [vector] * 4,
+        [field] + work, None, {4 + k: k for k in range(3)},
+    )
+    got = [mt_a, along_time(mt, 0, True), *along_z(mz)]
+
+    def neighbours(colour, e, base, fields=()):
+        outs = [vector, pair] if fields else [vector]
+        return call(functools.partial(local_kernel, colour), [e, base, time0, *fields], outs, work)
+
+    (r,) = neighbours(0, e, r)
     blocks = [m0, m1]
     x = [e, None]
     kept = [s0, None]
     last = 2 * SWEEPS - 1
     for index in range(1, last + 1):
         colour = index % 2
-        ins = [steps, r, mt_in, *mz_in, blocks[colour], time1]
+        ins = [steps, r, *got, blocks[colour], time1]
         fresh = x[colour] is None
         if not fresh:
             ins.append(x[colour])
-        e, kept[colour], x[colour], mt, mz = call(
-            functools.partial(sweep_kernel, colour, n_z, fresh), "sweep", [VMEM] * len(ins), [vector] * 5, [field] + work
-        )(*ins)
-        mt_in, mz_in = exchange(colour, mt, mz)
-        r = neighbours(colour, e, kept[1 - colour])
+        kernel = functools.partial(sweep_kernel, colour, len(got) - n_z, n_z, fresh)
+        e, kept[colour], x[colour], mz, mt = call(kernel, ins, [vector] * 5, [field] + work)
+        got = [along_time(mt, colour), *along_z(mz)]
+        fields = (x[colour], x[1 - colour]) if index == last else ()
+        r, *sol = neighbours(colour, e, kept[1 - colour], fields)
     colour = (last + 1) % 2
-    ins = [r, mt_in, *mz_in, blocks[colour], time1, kept[1 - colour], x[colour], x[1 - colour]]
-    sol, res = call(functools.partial(last_kernel, colour, n_z), "last", [VMEM] * len(ins), [pair, pair], [ab, part])(*ins)
-    return sol.reshape(rhs.shape), res.reshape(rhs.shape)
+    ins = [r, *got, blocks[colour], time1, kept[1 - colour]]
+    (res,) = call(functools.partial(last_kernel, colour, n_z), ins, [pair], [ab, part])
+    return sol[0].reshape(rhs.shape), res.reshape(rhs.shape)
 
 
 def solution(mesh):

time: 50.4 us -> 45.7 us (0.907)
  Pallas kernels: 23.2 us -> 16.7 us
  starting transfers between devices: 9.98 us -> 11.7 us
    pallas_call x9 -> x12, Pallas kernels: 23.2 us -> 16.7 us  [call(): pl.pallas_call(kernel, in_specs=specs or [VMEM] * len(ins), out_specs=[VM...]
    ppermute x8 -> x9, starting transfers between devices: 9.98 us -> 11.7 us  [the longest x5 9.58 us: along_time(): return lax.ppermute(mt, ('ta', 'sa'), time_pairs(colour, late))]
    ppermute x8 -> x9, waiting for transfers between devices: 16.4 us -> 16.3 us  [the longest x5 16.3 us: along_time(): return lax.ppermute(mt, ('ta', 'sa'), time_pairs(colour, late))]
  transfers between devices with their start and end apart: 8 -> 9, of which waited for: 4 -> 4; matrix products, arithmetic and copies ran while one was open for 0% -> 0% of each run, Pallas kernels for 2% -> 4%
where the time goes in v1:
time: 45.7 us; the launch traced here: 45.5 us
  Pallas kernels  16.7 us (37%)
  waiting for transfers between devices  16.3 us (36%)
  starting transfers between devices  11.7 us (26%)
  between operations  0.74 us (2%)
    pallas_call x12, Pallas kernels, call(): pl.pallas_call(kernel, in_specs=specs or [VMEM] * len(ins), out_specs=[VM...  16.7 us
    ppermute x5, waiting for transfers between devices, along_time(): return lax.ppermute(mt, ('ta', 'sa'), time_pairs(colour, late))  16.3 us
    ppermute x5, starting transfers between devices, along_time(): return lax.ppermute(mt, ('ta', 'sa'), time_pairs(colour, late))  9.58 us
    ppermute x4, starting transfers between devices, along_z(): got = [lax.ppermute(mz, 'sa', [(s, (s - 1) % n_s) for s in range(n_s)])]  2.16 us
  transfers between devices with their start and end apart: 9, of which 4 were waited for; matrix products, arithmetic and copies ran while one was open for 0% of the time, Pallas kernels for 4%

profile of v1, /device:TPU:0, one launch (start us, length us, event | category | flops | bytes accessed | tf_op | source)
XLA Modules:
  0.0 45.5 jit_solution(378347277020915448)
XLA Ops:
  0.6 3.4 %shard_map.59 = (bf16[4,20,80,128]{3,2,1,0:T(8,128)(2,1)S(1)}, bf16[20,80,128]{2,1,0:T(8,128)(2,1)S(1)}, bf16[4,20,80,128]{3,2,1,0:T(8,128)(2,1)S(1)}, bf16[20,8...) custom-call(s32[1,1,2]{2,1,0:T(1,128)} %refs_0_.3, ...), custom_call_target="tpu_custom_call" | custom-call | tf_op jit(solution)/shard_map/pallas_call | solution.py:458
  4.0 2.5 %shard_map.61 = (f32[40,128]{1,0:T(8,128)S(1)}, f32[40,128]{1,0:T(8,128)S(1)}, f32[40,128]{1,0:T(8,128)S(1)}, f32[40,128]{1,0:T(8,128)S(1)}) custom-call(f32[2,8,128]{2,1,0:T(8,128)S(1)} %get-tuple-element.47.refs_10_.steps_ref, f32[40,128]{1,0:T(8,128)S(1)} %get-tuple-element.45.refs_8_.r_ref, bf16[4,20,80,128]{3,2,1,0:T(8,128)(2,1)S(1)} %get-tuple-element.41.refs_4_.m_ref, ...), custom_call_target="tpu_custom_call" | custom-call | tf_op jit(solution)/shard_map/pallas_call | solution.py:458
  6.5 0.2 shard_map.60
  6.8 0.7 %collective-permute-start.1 = (f32[40,128]{1,0:T(8,128)S(1)}, f32[40,128]{1,0:T(8,128)S(1)}, u32[]{:S(2)}, u32[]{:S(2)}) collective-permute-start(f32[40,128]{1,0:T(8,128)S(1)} %get-tuple-element.59), channel_id=1, source_target_pairs={{0,1},{1,3},{2,0},{3,2},{4,5},{5,7},{6,4},{7,6},{8,9},{9,11},{10,8... | collective-permute-start | bytes 61448 | tf_op jit(solution)/shard_map/ppermute | solution.py:481
  7.4 2.0 %collective-permute-start.2 = (f32[40,128]{1,0:T(8,128)S(1)}, f32[40,128]{1,0:T(8,128)S(1)}, u32[]{:S(2)}, u32[]{:S(2)}) collective-permute-start(f32[40,128]{1,0:T(8,128)S(1)} %get-tuple-element.60), channel_id=1, source_target_pairs={{0,1},{1,0},{2,3},{3,2},{4,5},{5,4},{6,7},{7,6},{8,9},{9,8},{10,11... | collective-permute-start | bytes 61448 | tf_op jit(solution)/shard_map/ppermute | solution.py:484
  9.4 6.7 %collective-permute-start = (f32[40,128]{1,0:T(8,128)S(1)}, f32[40,128]{1,0:T(8,128)S(1)}, u32[]{:S(2)}, u32[]{:S(2)}) collective-permute-start(f32[40,128]{1,0:T(8,128)S(1)} %get-tuple-element.58), channel_id=1, source_target_pairs={{0,30},{3,5},{4,2},{7,9},{8,6},{11,13},{12,10},{15,17},{16,14},{19... | collective-permute-start | bytes 61448 | tf_op jit(solution)/shard_map/ppermute | solution.py:481
  16.2 0.2 shard_map.63.refs_1_
  16.4 0.0 collective-permute-done.1.refs_3_
  16.4 0.0 collective-permute-done.2.refs_4_
  16.4 1.3 %collective-permute-done.refs_2_ = f32[40,128]{1,0:T(8,128)S(1)} collective-permute-done((f32[40,128]{1,0:T(8,128)S(1)}, f32[40,128]{1,0:T(8,128)S(1)}, u32[]{:S(2)}, u32[]{:S(2)}) %collective-permute-start) | collective-permute-done | bytes 20512 | tf_op jit(solution)/shard_map/ppermute | solution.py:481
  17.6 2.7 %shard_map.64 = (f32[40,128]{1,0:T(8,128)S(1)}, f32[40,128]{1,0:T(8,128)S(1)}, f32[40,128]{1,0:T(8,128)S(1)}, f32[40,128]{1,0:T(8,128)S(1)}, f32[40,128]{1,0:T(8,128)S(1)}) custom-call(f32[2,8,128]{2,1,0:T(8,128)S(1)} %get-tuple-element.48.steps_ref.refs_0_, f32[40,128]{1,0:T(8,128)S(1)} %shard_map.63.refs_1_, f32[40,128]{1,0:T(8,128)S(1)} %collective-permute-done.refs_2_, ...), custom_call_target="tpu_custom_call" | custom-call | tf_op jit(solution)/shard_map/pallas_call | solution.py:458
  20.3 0.1 collective-permute-start.3
  20.4 0.1 collective-permute-start.4
  20.5 0.3 shard_map.65.refs_1_
  20.8 7.2 %collective-permute-done.3.refs_2_ = f32[40,128]{1,0:T(8,128)S(1)} collective-permute-done((f32[40,128]{1,0:T(8,128)S(1)}, f32[40,128]{1,0:T(8,128)S(1)}, u32[]{:S(2)}, u32[]{:S(2)}) %collective-permute-start.3) | collective-permute-done | bytes 20512 | tf_op jit(solution)/shard_map/ppermute | solution.py:481
  28.0 0.0 collective-permute-done.4.refs_3_
  28.0 2.5 %shard_map.66 = (f32[40,128]{1,0:T(8,128)S(1)}, f32[40,128]{1,0:T(8,128)S(1)}, f32[40,128]{1,0:T(8,128)S(1)}, f32[40,128]{1,0:T(8,128)S(1)}, f32[40,128]{1,0:T(8,128)S(1)}) custom-call(f32[2,8,128]{2,1,0:T(8,128)S(1)} %get-tuple-element.48.steps_ref.refs_0_, f32[40,128]{1,0:T(8,128)S(1)} %shard_map.65.refs_1_, f32[40,128]{1,0:T(8,128)S(1)} %collective-permute-done.3.refs_2_, ...), custom_call_target="tpu_custom_call" | custom-call | tf_op jit(solution)/shard_map/pallas_call | solution.py:458
  30.6 2.1 %collective-permute-start.5 = (f32[40,128]{1,0:T(8,128)S(1)}, f32[40,128]{1,0:T(8,128)S(1)}, u32[]{:S(2)}, u32[]{:S(2)}) collective-permute-start(f32[40,128]{1,0:T(8,128)S(1)} %get-tuple-element.68), channel_id=1, source_target_pairs={{0,30},{1,3},{2,0},{3,5},{4,2},{5,7},{6,4},{7,9},{8,6},{9,11},{10,... | collective-permute-start | bytes 61448 | tf_op jit(solution)/shard_map/ppermute | solution.py:481
  32.6 0.0 collective-permute-start.6
  32.6 0.2 shard_map.67.refs_1_
  32.8 1.6 %collective-permute-done.5.refs_2_ = f32[40,128]{1,0:T(8,128)S(1)} collective-permute-done((f32[40,128]{1,0:T(8,128)S(1)}, f32[40,128]{1,0:T(8,128)S(1)}, u32[]{:S(2)}, u32[]{:S(2)}) %collective-permute-start.5) | collective-permute-done | bytes 20512 | tf_op jit(solution)/shard_map/ppermute | solution.py:481
  34.4 0.0 collective-permute-done.6.refs_3_
  34.4 2.7 %shard_map.68 = (f32[40,128]{1,0:T(8,128)S(1)}, f32[40,128]{1,0:T(8,128)S(1)}, f32[40,128]{1,0:T(8,128)S(1)}, f32[40,128]{1,0:T(8,128)S(1)}, f32[40,128]{1,0:T(8,128)S(1)}) custom-call(f32[2,8,128]{2,1,0:T(8,128)S(1)} %get-tuple-element.48.steps_ref.refs_0_, f32[40,128]{1,0:T(8,128)S(1)} %shard_map.67.refs_1_, f32[40,128]{1,0:T(8,128)S(1)} %collective-permute-done.5.refs_2_, ...), custom_call_target="tpu_custom_call" | custom-call | tf_op jit(solution)/shard_map/pallas_call | solution.py:458
  37.1 0.1 collective-permute-start.7
  37.1 0.1 collective-permute-start.8
  37.2 1.0 %shard_map.69 = (f32[40,128]{1,0:T(8,128)S(1)}, f32[2,40,128]{2,1,0:T(8,128)}) custom-call(f32[40,128]{1,0:T(8,128)S(1)} %get-tuple-element.71.e_ref, f32[40,128]{1,0:T(8,128)S(1)} %get-tuple-element.72.s_ref, bf16[20,80,128]{2,1,0:T(8,128)(2,1)S(1)} %get-tuple-element.57.time_ref, f32[40,128]{1,0:T(8,128)S(1)} %get-tuple-element.73.refs_0_, ...), custom_call_target="tpu_custom_call" | custom-call | tf_op jit(solution)/shard_map/pallas_call | solution.py:458
  38.2 6.3 %collective-permute-done.7.refs_0_ = f32[40,128]{1,0:T(8,128)S(1)} collective-permute-done((f32[40,128]{1,0:T(8,128)S(1)}, f32[40,128]{1,0:T(8,128)S(1)}, u32[]{:S(2)}, u32[]{:S(2)}) %collective-permute-start.7) | collective-permute-done | bytes 20512 | tf_op jit(solution)/shard_map/ppermute | solution.py:481
  44.5 0.0 collective-permute-done.8.refs_1_
  44.5 1.0 %shard_map.70 = f32[2,40,128]{2,1,0:T(8,128)} custom-call(f32[40,128]{1,0:T(8,128)S(1)} %get-tuple-element.76.r_ref, f32[40,128]{1,0:T(8,128)S(1)} %collective-permute-done.7.refs_0_, f32[40,128]{1,0:T(8,128)S(1)} %collective-permute-done.8.refs_1_, bf16[4,20,80,128]{3,2,1,0:T(8,128)(2,1)S(1)} %get-tuple-element.50.m_ref.refs_4_.refs_2_, ...), custom_call_target="tpu_custom_call" | custom-call | tf_op jit(solution)/shard_map/pallas_call | solution.py:458
  (1 shorter events, 0.0 us)
Async XLA Ops:
  6.8 9.6 %collective-permute-start.1 = (f32[40,128]{1,0:T(8,128)S(1)}, f32[40,128]{1,0:T(8,128)S(1)}, u32[]{:S(2)}, u32[]{:S(2)}) collective-permute-start(f32[40,128]{1,0:T(8,128)S(1)} %get-tuple-element.59), channel_id=1, source_target_pairs={{0,1},{1,3},{2,0},{3,2},{4,5},{5,7},{6,4},{7,6},{8,9},{9,11},{10,8... | collective-permute-start | bytes 61448 | tf_op jit(solution)/shard_map/ppermute | solution.py:481
  7.4 9.0 %collective-permute-start.2 = (f32[40,128]{1,0:T(8,128)S(1)}, f32[40,128]{1,0:T(8,128)S(1)}, u32[]{:S(2)}, u32[]{:S(2)}) collective-permute-start(f32[40,128]{1,0:T(8,128)S(1)} %get-tuple-element.60), channel_id=1, source_target_pairs={{0,1},{1,0},{2,3},{3,2},{4,5},{5,4},{6,7},{7,6},{8,9},{9,8},{10,11... | collective-permute-start | bytes 61448 | tf_op jit(solution)/shard_map/ppermute | solution.py:484
  9.4 8.2 %collective-permute-start = (f32[40,128]{1,0:T(8,128)S(1)}, f32[40,128]{1,0:T(8,128)S(1)}, u32[]{:S(2)}, u32[]{:S(2)}) collective-permute-start(f32[40,128]{1,0:T(8,128)S(1)} %get-tuple-element.58), channel_id=1, source_target_pairs={{0,30},{3,5},{4,2},{7,9},{8,6},{11,13},{12,10},{15,17},{16,14},{19... | collective-permute-start | bytes 61448 | tf_op jit(solution)/shard_map/ppermute | solution.py:481
  20.3 7.7 %collective-permute-start.3 = (f32[40,128]{1,0:T(8,128)S(1)}, f32[40,128]{1,0:T(8,128)S(1)}, u32[]{:S(2)}, u32[]{:S(2)}) collective-permute-start(f32[40,128]{1,0:T(8,128)S(1)} %get-tuple-element.64), channel_id=1, source_target_pairs={{0,2},{1,31},{2,4},{3,1},{4,6},{5,3},{6,8},{7,5},{8,10},{9,7},{10,... | collective-permute-start | bytes 61448 | tf_op jit(solution)/shard_map/ppermute | solution.py:481
  20.4 7.6 %collective-permute-start.4 = (f32[40,128]{1,0:T(8,128)S(1)}, f32[40,128]{1,0:T(8,128)S(1)}, u32[]{:S(2)}, u32[]{:S(2)}) collective-permute-start(f32[40,128]{1,0:T(8,128)S(1)} %get-tuple-element.65), channel_id=1, source_target_pairs={{0,1},{1,0},{2,3},{3,2},{4,5},{5,4},{6,7},{7,6},{8,9},{9,8},{10,11... | collective-permute-start | bytes 61448 | tf_op jit(solution)/shard_map/ppermute | solution.py:484
  30.6 3.8 %collective-permute-start.5 = (f32[40,128]{1,0:T(8,128)S(1)}, f32[40,128]{1,0:T(8,128)S(1)}, u32[]{:S(2)}, u32[]{:S(2)}) collective-permute-start(f32[40,128]{1,0:T(8,128)S(1)} %get-tuple-element.68), channel_id=1, source_target_pairs={{0,30},{1,3},{2,0},{3,5},{4,2},{5,7},{6,4},{7,9},{8,6},{9,11},{10,... | collective-permute-start | bytes 61448 | tf_op jit(solution)/shard_map/ppermute | solution.py:481
  32.6 1.8 %collective-permute-start.6 = (f32[40,128]{1,0:T(8,128)S(1)}, f32[40,128]{1,0:T(8,128)S(1)}, u32[]{:S(2)}, u32[]{:S(2)}) collective-permute-start(f32[40,128]{1,0:T(8,128)S(1)} %get-tuple-element.69), channel_id=1, source_target_pairs={{0,1},{1,0},{2,3},{3,2},{4,5},{5,4},{6,7},{7,6},{8,9},{9,8},{10,11... | collective-permute-start | bytes 61448 | tf_op jit(solution)/shard_map/ppermute | solution.py:484
  37.1 7.4 %collective-permute-start.7 = (f32[40,128]{1,0:T(8,128)S(1)}, f32[40,128]{1,0:T(8,128)S(1)}, u32[]{:S(2)}, u32[]{:S(2)}) collective-permute-start(f32[40,128]{1,0:T(8,128)S(1)} %get-tuple-element.77), channel_id=1, source_target_pairs={{0,2},{1,31},{2,4},{3,1},{4,6},{5,3},{6,8},{7,5},{8,10},{9,7},{10,... | collective-permute-start | bytes 61448 | tf_op jit(solution)/shard_map/ppermute | solution.py:481
  37.1 7.4 %collective-permute-start.8 = (f32[40,128]{1,0:T(8,128)S(1)}, f32[40,128]{1,0:T(8,128)S(1)}, u32[]{:S(2)}, u32[]{:S(2)}) collective-permute-start(f32[40,128]{1,0:T(8,128)S(1)} %get-tuple-element.78), channel_id=1, source_target_pairs={{0,1},{1,0},{2,3},{3,2},{4,5},{5,4},{6,7},{7,6},{8,9},{9,8},{10,11... | collective-permute-start | bytes 61448 | tf_op jit(solution)/shard_map/ppermute | solution.py:484

commit v2 on v1

--- a/solution.py
+++ b/solution.py
@@ -15,7 +15,7 @@
 SWEEPS = 2
 PLANE = LY * LX
 UNIT = 4
-PIECES = 2
+PIECES = 1
 
 F32 = jnp.float32
 BF16 = jnp.bfloat16
@@ -70,7 +70,7 @@
     edge = place // stride % extent == (extent - 1 if sign > 0 else 0)
     inner = turn(x, extra - sign * stride)
     if direction == 1:
-        return jnp.where(edge, 0.0, inner)
+        return jnp.where(edge, jnp.zeros_like(inner), inner)
     return jnp.where(edge, turn(x, extra + sign * (extent - 1) * stride), inner)
 
 
@@ -129,7 +129,7 @@
             spread_ref[kind, k, r] = jnp.broadcast_to(rows_ref[k, row:row + 1, :], (16, width)).astype(BF16)
 
 
-def forward_sums(terms, ab_ref, part_ref, unroll=1):
+def forward_sums(terms, ab_ref, part_ref, unroll=1, start=0):
     entries, rows, _ = terms[0][0].shape
 
     def body(group, carry):
@@ -139,35 +139,32 @@
                 total = None
                 for m_ref, slot in terms:
                     for t in range(0, rows, 16):
-                        m = m_ref[r, pl.ds(t, 16), :].astype(F32)
+                        m = m_ref[r + start, pl.ds(t, 16), :].astype(F32)
                         for k in range(2):
                             product = m * ab_ref[slot, kind, k, pl.ds(t, 16), :].astype(F32)
                             total = product if total is None else total + product
-                part_ref[kind, r] = total[:8] + total[8:]
+                part_ref[kind, r] = total
         return carry
 
     lax.fori_loop(0, entries // 2, body, 0, unroll=unroll)
     out = []
     for t in range(0, entries, UNIT):
-        parts = [part_ref[kind, t + k] for kind in range(2) for k in range(UNIT)]
+        parts = [part_ref[kind, t + k, 0:8, :] + part_ref[kind, t + k, 8:16, :] for kind in range(2) for k in range(UNIT)]
         out.append(gather_rows(parts))
     return jnp.concatenate(out, 0)
 
 
 def backward_sums(m_ref, spread_ref, back_ref):
     entries, rows, _ = m_ref.shape
-    starts = list(range(0, rows, 16))
-    for pair in [starts[k:k + 2] for k in range(0, len(starts), 2)]:
-        for t in pair:
-            for kind in range(2):
-                totals = [None] * (2 if len(pair) == 1 else 1)
-                for r in range(entries):
-                    m = m_ref[r, pl.ds(t, 16), :].astype(F32)
-                    for k in range(2):
-                        product = m * spread_ref[kind, k, r].astype(F32)
-                        slot = k % len(totals)
-                        totals[slot] = product if totals[slot] is None else totals[slot] + product
-                back_ref[kind, pl.ds(t, 16), :] = totals[0] if len(totals) == 1 else totals[0] + totals[1]
+    for t in range(0, rows, 16):
+        for kind in range(2):
+            total = None
+            for r in range(entries):
+                m = m_ref[r, pl.ds(t, 16), :].astype(F32)
+                for k in range(2):
+                    product = m * spread_ref[kind, k, r].astype(F32)
+                    total = product if total is None else total + product
+            back_ref[kind, pl.ds(t, 16), :] = total
 
 
 def backward_halves(back_ref):
@@ -182,16 +179,19 @@
     return jnp.concatenate(a, 0), jnp.concatenate(b, 0)
 
 
-def block_operator(x, unroll, m_ref, ab_ref, rows_ref, spread_ref, back_ref, part_ref):
+def block_operator(x, unroll, start, m_ref, ab_ref, rows_ref, spread_ref, back_ref, part_ref):
     half = x.shape[1] // 2
     put_forward(x, swap(x), ab_ref, 0)
-    for direction in (1, 2, 3):
-        put_forward(-shifted(x, direction, 1, 0), -shifted(x, direction, 1, half), ab_ref, direction)
+    for kind in range(2):
+        for k in range(2):
+            hopped = -ab_ref[0, kind, k]
+            for direction in (1, 2, 3):
+                ab_ref[direction, kind, k] = shifted(hopped, direction, 1, 0)
     put_backward(x, rows_ref, spread_ref)
 
     for direction in (1, 2, 3):
         backward_sums(m_ref.at[direction], spread_ref, back_ref.at[direction])
-    total = forward_sums([(m_ref.at[term], term) for term in range(4)], ab_ref, part_ref, unroll)
+    total = forward_sums([(m_ref.at[term], term) for term in range(4)], ab_ref, part_ref, unroll, start)
     backs = 0.0
     for direction in (1, 2, 3):
         a, b = backward_halves(back_ref.at[direction])
@@ -222,16 +222,17 @@
     return jnp.concatenate([alpha * tile for tile in tiles(x)], 0)
 
 
-def relax(residual, steps, m_ref, s_ref, e_ref, w_ref, work, mine=None):
+def relax(residual, steps, m_ref, s_ref, e_ref, w_ref, work, mine=None, trips=4):
     @pl.when(True if mine is None else mine)
     def _():
-        s_ref[...] = residual
-        e_ref[...] = jnp.zeros_like(residual)
-        w_ref[...] = jnp.zeros_like(residual)
+        if residual is not None:
+            s_ref[...] = residual
+        e_ref[...] = jnp.zeros_like(e_ref)
+        w_ref[...] = jnp.zeros_like(w_ref)
 
     def step(index, carry):
         s = s_ref[...]
-        q, back_z = block_operator(s, s.shape[0] // (4 if mine is None else 8), m_ref, *work)
+        q, back_z = block_operator(s, s.shape[0] // trips, jnp.minimum(index, 0), m_ref, *work)
         s = s_ref[...]
         i_s = times_i(s)
         scale = total_of(q * q) + 1e-6
@@ -309,8 +310,8 @@
     return copies
 
 
-def first_turn(late):
-    early = lax.axis_index("ta") % 2 == which(0)
+def turn_of(colour, late):
+    early = lax.axis_index("ta") % 2 == which(colour)
     return jnp.logical_not(early) if late else early
 
 
@@ -322,7 +323,7 @@
      raw_ref, rhs_ref, count_ref, sem) = refs
     half = which(0)
 
-    @pl.when(first_turn(late))
+    @pl.when(turn_of(0, late))
     def _():
         dof = rhs_ref.shape[1]
         pieces = []
@@ -340,12 +341,13 @@
                 pack_matrix(raw_ref.at[term], 1, time_ref, time_other_ref)
             else:
                 pack_matrix(raw_ref.at[term], half, m_ref.at[term], m_other_ref.at[term])
-        copies[-2].wait()
-        copies[-1].wait()
-        for k in range(2):
-            steps_ref[k] = jnp.full(steps_ref.shape[1:], count_ref[0, 0, k].astype(F32))
-        own_ref[...] = pack_field(rhs_ref, half)
-        other_ref[...] = pack_field(rhs_ref, 1 - half)
+            if term == 1:
+                copies[-2].wait()
+                copies[-1].wait()
+                for k in range(2):
+                    steps_ref[k] = jnp.full(steps_ref.shape[1:], count_ref[0, 0, k].astype(F32))
+                own_ref[...] = pack_field(rhs_ref, half)
+                other_ref[...] = pack_field(rhs_ref, 1 - half)
 
 
 def first_kernel(late, steps_ref, r_ref, m_ref, time_ref, *refs):
@@ -354,8 +356,8 @@
     e_ref, s_ref, mz_ref, mt_ref, w_ref, *work = refs
     _, rows_ref, spread_ref, back_ref, _ = work
     half = which(0)
-    mine = first_turn(late)
-    relax(r_ref[...], steps_ref[half], m_ref, s_ref, e_ref, w_ref, work, mine)
+    mine = turn_of(0, late)
+    relax(r_ref[...], steps_ref[half], m_ref, s_ref, e_ref, w_ref, work, mine, 8)
 
     @pl.when(mine)
     def _():
@@ -394,31 +396,44 @@
     return total + forward_sums([(m_ref.at[1], 0), (time_ref, 1)], ab_ref, part_ref)
 
 
-def sweep_kernel(colour, n_t_in, n_z, fresh, *refs):
+def sweep_kernel(colour, n_t_in, n_z, fresh, late, *refs):
     steps_ref, r_ref, *refs = refs
-    mt, mz_up, mz_down, refs = arrivals(refs, n_t_in, n_z)
+    arrived = refs
+    refs = refs[n_t_in + n_z:]
     m_ref, time_ref, *refs = refs
     if not fresh:
         sol_ref, *refs = refs
+    if late:
+        refs = refs[4:]
     e_ref, s_ref, new_ref, mz_ref, mt_ref, w_ref, *work = refs
     ab_ref, rows_ref, spread_ref, back_ref, part_ref = work
     half = which(colour)
-    residual = remote_part(half, r_ref[...], mt, mz_up, mz_down, m_ref, time_ref, ab_ref, part_ref)
-    relax(residual, steps_ref[half], m_ref, s_ref, e_ref, w_ref, work)
-    send(half, e_ref[...], w_ref, mt_ref, mz_ref, time_ref, rows_ref, spread_ref, back_ref)
-    new_ref[...] = e_ref[...] if fresh else sol_ref[...] + e_ref[...]
-
-
-def arrivals(refs, n_t_in, n_z):
+    mine = None if late is None else turn_of(colour, late)
+    always = True if late is None else mine
+
+    @pl.when(always)
+    def _():
+        mt, mz_up, mz_down, _ = arrivals(arrived, colour, n_t_in, n_z)
+        s_ref[...] = remote_part(half, r_ref[...], mt, mz_up, mz_down, m_ref, time_ref, ab_ref, part_ref)
+
+    relax(None, steps_ref[half], m_ref, s_ref, e_ref, w_ref, work, mine)
+
+    @pl.when(always)
+    def _():
+        send(half, e_ref[...], w_ref, mt_ref, mz_ref, time_ref, rows_ref, spread_ref, back_ref)
+        new_ref[...] = e_ref[...] if fresh else sol_ref[...] + e_ref[...]
+
+
+def arrivals(refs, colour, n_t_in, n_z):
     mt = refs[0][...]
     if n_t_in == 2:
-        mt = jnp.where(first_turn(False), refs[1][...], mt)
+        mt = jnp.where(turn_of(1 - colour, False), refs[1][...], mt)
     up, down = refs[n_t_in], refs[n_t_in + n_z - 1]
     return mt, up[...], down[...], refs[n_t_in + n_z:]
 
 
-def last_kernel(colour, n_z, r_ref, *refs):
-    mt, mz_up, mz_down, refs = arrivals(refs, 1, n_z)
+def last_kernel(colour, n_t_in, n_z, r_ref, *refs):
+    mt, mz_up, mz_down, refs = arrivals(refs, colour, n_t_in, n_z)
     m_ref, time_ref, s_ref, res_ref, ab_ref, part_ref = refs
     half = which(colour)
     residual = remote_part(half, r_ref[...], mt, mz_up, mz_down, m_ref, time_ref, ab_ref, part_ref)
@@ -442,7 +457,7 @@
     pair = jax.ShapeDtypeStruct((2, dof, width), F32)
     field = pltpu.VMEM((dof, width), F32)
     ab = pltpu.VMEM((4, 2, 2, 2 * dof, width), BF16)
-    part = pltpu.VMEM((2, dof // 2, 8, width), F32)
+    part = pltpu.VMEM((2, dof // 2, 16, width), F32)
     work = [
         ab,
         pltpu.VMEM((2, dof, width), F32),
@@ -519,13 +534,23 @@
         if not fresh:
             ins.append(x[colour])
         kernel = functools.partial(sweep_kernel, colour, len(got) - n_z, n_z, fresh)
-        e, kept[colour], x[colour], mz, mt = call(kernel, ins, [vector] * 5, [field] + work)
-        got = [along_time(mt, colour), *along_z(mz)]
+        outs = [vector] * 5
+        if index == 1:
+            early = call(functools.partial(kernel, False), ins, outs, [field] + work)
+            mt_a = along_time(early[-1], colour, False)
+            e, kept[colour], x[colour], mz, mt = call(
+                functools.partial(kernel, True), [*ins, *early[:-1]], outs, [field] + work,
+                None, {len(ins) + k: k for k in range(4)},
+            )
+            got = [mt_a, along_time(mt, colour, True), *along_z(mz)]
+        else:
+            e, kept[colour], x[colour], mz, mt = call(functools.partial(kernel, None), ins, outs, [field] + work)
+            got = [along_time(mt, colour), *along_z(mz)]
         fields = (x[colour], x[1 - colour]) if index == last else ()
         r, *sol = neighbours(colour, e, kept[1 - colour], fields)
     colour = (last + 1) % 2
     ins = [r, *got, blocks[colour], time1, kept[1 - colour]]
-    (res,) = call(functools.partial(last_kernel, colour, n_z), ins, [pair], [ab, part])
+    (res,) = call(functools.partial(last_kernel, colour, len(got) - n_z, n_z), ins, [pair], [ab, part])
     return sol[0].reshape(rhs.shape), res.reshape(rhs.shape)
 
 

time: 45.7 us -> 47.7 us (1.044)
  starting transfers between devices: 11.7 us -> 14.8 us
  waiting for transfers between devices: 16.3 us -> 15.4 us
    ppermute x4, starting transfers between devices: 2.16 us -> 5.98 us  [along_z(): got = [lax.ppermute(mz, 'sa', [(s, (s - 1) % n_s) for s in range(n_s)])]]
    ppermute x5 -> x6, waiting for transfers between devices: 16.3 us -> 15.4 us  [along_time(): return lax.ppermute(mt, ('ta', 'sa'), time_pairs(colour, late))]
    ppermute x5 -> x6, starting transfers between devices: 9.58 us -> 8.77 us  [along_time(): return lax.ppermute(mt, ('ta', 'sa'), time_pairs(colour, late))]
    pallas_call x12 -> x13, Pallas kernels: 16.7 us -> 16.6 us  [call(): pl.pallas_call(kernel, in_specs=specs or [VMEM] * len(ins), out_specs=[VM...]
  transfers between devices with their start and end apart: 9 -> 10, of which waited for: 4 -> 4; matrix products, arithmetic and copies ran while one was open for 0% -> 0% of each run, Pallas kernels for 4% -> 4%
where the time goes in v2:
time: 47.7 us; the launch traced here: 47.5 us
  Pallas kernels  16.6 us (35%)
  waiting for transfers between devices  15.4 us (32%)
  starting transfers between devices  14.8 us (31%)
  between operations  0.75 us (2%)
    pallas_call x13, Pallas kernels, call(): pl.pallas_call(kernel, in_specs=specs or [VMEM] * len(ins), out_specs=[VM...  16.6 us
    ppermute x6, waiting for transfers between devices, along_time(): return lax.ppermute(mt, ('ta', 'sa'), time_pairs(colour, late))  15.4 us
    ppermute x6, starting transfers between devices, along_time(): return lax.ppermute(mt, ('ta', 'sa'), time_pairs(colour, late))  8.77 us
    ppermute x4, starting transfers between devices, along_z(): got = [lax.ppermute(mz, 'sa', [(s, (s - 1) % n_s) for s in range(n_s)])]  5.98 us
  transfers between devices with their start and end apart: 10, of which 4 were waited for; matrix products, arithmetic and copies ran while one was open for 0% of the time, Pallas kernels for 4%

profile of v2, /device:TPU:0, one launch (start us, length us, event | category | flops | bytes accessed | tf_op | source)
XLA Modules:
  0.0 47.5 jit_solution(6842338995992500594)
XLA Ops:
  0.6 3.3 %shard_map.59 = (bf16[4,20,80,128]{3,2,1,0:T(8,128)(2,1)S(1)}, bf16[20,80,128]{2,1,0:T(8,128)(2,1)S(1)}, bf16[4,20,80,128]{3,2,1,0:T(8,128)(2,1)S(1)}, bf16[20,8...) custom-call(s32[1,1,2]{2,1,0:T(1,128)} %refs_0_.3, ...), custom_call_target="tpu_custom_call" | custom-call | tf_op jit(solution)/shard_map/pallas_call | solution.py:473
  3.9 2.4 %shard_map.61 = (f32[40,128]{1,0:T(8,128)S(1)}, f32[40,128]{1,0:T(8,128)S(1)}, f32[40,128]{1,0:T(8,128)S(1)}, f32[40,128]{1,0:T(8,128)S(1)}) custom-call(f32[2,8,128]{2,1,0:T(8,128)S(1)} %get-tuple-element.52.refs_10_.steps_ref, f32[40,128]{1,0:T(8,128)S(1)} %get-tuple-element.50.refs_8_.r_ref, bf16[4,20,80,128]{3,2,1,0:T(8,128)(2,1)S(1)} %get-tuple-element.46.refs_4_.m_ref, ...), custom_call_target="tpu_custom_call" | custom-call | tf_op jit(solution)/shard_map/pallas_call | solution.py:473
  6.4 0.1 shard_map.60
  6.5 0.7 %collective-permute-start.1 = (f32[40,128]{1,0:T(8,128)S(1)}, f32[40,128]{1,0:T(8,128)S(1)}, u32[]{:S(2)}, u32[]{:S(2)}) collective-permute-start(f32[40,128]{1,0:T(8,128)S(1)} %get-tuple-element.64), channel_id=1, source_target_pairs={{0,1},{1,3},{2,0},{3,2},{4,5},{5,7},{6,4},{7,6},{8,9},{9,11},{10,8... | collective-permute-start | bytes 61448 | tf_op jit(solution)/shard_map/ppermute | solution.py:496
  7.2 2.0 %collective-permute-start.2 = (f32[40,128]{1,0:T(8,128)S(1)}, f32[40,128]{1,0:T(8,128)S(1)}, u32[]{:S(2)}, u32[]{:S(2)}) collective-permute-start(f32[40,128]{1,0:T(8,128)S(1)} %get-tuple-element.65), channel_id=1, source_target_pairs={{0,1},{1,0},{2,3},{3,2},{4,5},{5,4},{6,7},{7,6},{8,9},{9,8},{10,11... | collective-permute-start | bytes 61448 | tf_op jit(solution)/shard_map/ppermute | solution.py:499
  9.2 6.7 %collective-permute-start = (f32[40,128]{1,0:T(8,128)S(1)}, f32[40,128]{1,0:T(8,128)S(1)}, u32[]{:S(2)}, u32[]{:S(2)}) collective-permute-start(f32[40,128]{1,0:T(8,128)S(1)} %get-tuple-element.63), channel_id=1, source_target_pairs={{0,30},{3,5},{4,2},{7,9},{8,6},{11,13},{12,10},{15,17},{16,14},{19... | collective-permute-start | bytes 61448 | tf_op jit(solution)/shard_map/ppermute | solution.py:496
  16.0 0.2 shard_map.63.refs_1_
  16.1 0.0 collective-permute-done.1.refs_3_
  16.2 0.0 collective-permute-done.2.refs_4_
  16.2 1.3 %collective-permute-done.refs_2_ = f32[40,128]{1,0:T(8,128)S(1)} collective-permute-done((f32[40,128]{1,0:T(8,128)S(1)}, f32[40,128]{1,0:T(8,128)S(1)}, u32[]{:S(2)}, u32[]{:S(2)}) %collective-permute-start) | collective-permute-done | bytes 20512 | tf_op jit(solution)/shard_map/ppermute | solution.py:496
  17.4 2.7 %shard_map.65 = (f32[40,128]{1,0:T(8,128)S(1)}, f32[40,128]{1,0:T(8,128)S(1)}, f32[40,128]{1,0:T(8,128)S(1)}, f32[40,128]{1,0:T(8,128)S(1)}, f32[40,128]{1,0:T(8,128)S(1)}) custom-call(f32[2,8,128]{2,1,0:T(8,128)S(1)} %get-tuple-element.53.steps_ref.refs_0_, ...), custom_call_target="tpu_custom_call", output_to_operand_aliasing={{0}: (7, {}), {1}: (8, {}), {2}: (9, {}), {3}: (10, {})} | custom-call | tf_op jit(solution)/shard_map/pallas_call | solution.py:473
  20.1 0.0 collective-permute-start.4
  20.1 0.5 %collective-permute-start.5 = (f32[40,128]{1,0:T(8,128)S(1)}, f32[40,128]{1,0:T(8,128)S(1)}, u32[]{:S(2)}, u32[]{:S(2)}) collective-permute-start(f32[40,128]{1,0:T(8,128)S(1)} %get-tuple-element.75), channel_id=1, source_target_pairs={{0,1},{1,0},{2,3},{3,2},{4,5},{5,4},{6,7},{7,6},{8,9},{9,8},{10,11... | collective-permute-start | bytes 61448 | tf_op jit(solution)/shard_map/ppermute | solution.py:499
  20.6 1.3 %collective-permute-start.3 = (f32[40,128]{1,0:T(8,128)S(1)}, f32[40,128]{1,0:T(8,128)S(1)}, u32[]{:S(2)}, u32[]{:S(2)}) collective-permute-start(f32[40,128]{1,0:T(8,128)S(1)} %get-tuple-element.73), channel_id=1, source_target_pairs={{1,31},{2,4},{5,3},{6,8},{9,7},{10,12},{13,11},{14,16},{17,15},{18... | collective-permute-start | bytes 61448 | tf_op jit(solution)/shard_map/ppermute | solution.py:496
  21.9 0.3 shard_map.66.refs_1_
  22.3 0.0 collective-permute-done.4.refs_3_
  22.3 0.0 collective-permute-done.5.refs_4_
  22.3 7.6 %collective-permute-done.3.refs_2_ = f32[40,128]{1,0:T(8,128)S(1)} collective-permute-done((f32[40,128]{1,0:T(8,128)S(1)}, f32[40,128]{1,0:T(8,128)S(1)}, u32[]{:S(2)}, u32[]{:S(2)}) %collective-permute-start.3) | collective-permute-done | bytes 20512 | tf_op jit(solution)/shard_map/ppermute | solution.py:496
  29.9 2.5 %shard_map.67 = (f32[40,128]{1,0:T(8,128)S(1)}, f32[40,128]{1,0:T(8,128)S(1)}, f32[40,128]{1,0:T(8,128)S(1)}, f32[40,128]{1,0:T(8,128)S(1)}, f32[40,128]{1,0:T(8,128)S(1)}) custom-call(f32[2,8,128]{2,1,0:T(8,128)S(1)} %get-tuple-element.53.steps_ref.refs_0_, f32[40,128]{1,0:T(8,128)S(1)} %shard_map.66.refs_1_, f32[40,128]{1,0:T(8,128)S(1)} %collective-permute-done.3.refs_2_, ...), custom_call_target="tpu_custom_call" | custom-call | tf_op jit(solution)/shard_map/pallas_call | solution.py:473
  32.5 0.1 collective-permute-start.6
  32.5 0.1 collective-permute-start.7
  32.6 0.2 shard_map.68.refs_1_
  32.8 3.5 %collective-permute-done.6.refs_2_ = f32[40,128]{1,0:T(8,128)S(1)} collective-permute-done((f32[40,128]{1,0:T(8,128)S(1)}, f32[40,128]{1,0:T(8,128)S(1)}, u32[]{:S(2)}, u32[]{:S(2)}) %collective-permute-start.6) | collective-permute-done | bytes 20512 | tf_op jit(solution)/shard_map/ppermute | solution.py:496
  36.3 0.0 collective-permute-done.7.refs_3_
  36.3 2.7 %shard_map.69 = (f32[40,128]{1,0:T(8,128)S(1)}, f32[40,128]{1,0:T(8,128)S(1)}, f32[40,128]{1,0:T(8,128)S(1)}, f32[40,128]{1,0:T(8,128)S(1)}, f32[40,128]{1,0:T(8,128)S(1)}) custom-call(f32[2,8,128]{2,1,0:T(8,128)S(1)} %get-tuple-element.53.steps_ref.refs_0_, f32[40,128]{1,0:T(8,128)S(1)} %shard_map.68.refs_1_, f32[40,128]{1,0:T(8,128)S(1)} %collective-permute-done.6.refs_2_, ...), custom_call_target="tpu_custom_call" | custom-call | tf_op jit(solution)/shard_map/pallas_call | solution.py:473
  39.0 0.0 collective-permute-start.8
  39.1 3.4 %collective-permute-start.9 = (f32[40,128]{1,0:T(8,128)S(1)}, f32[40,128]{1,0:T(8,128)S(1)}, u32[]{:S(2)}, u32[]{:S(2)}) collective-permute-start(f32[40,128]{1,0:T(8,128)S(1)} %get-tuple-element.88), channel_id=1, source_target_pairs={{0,1},{1,0},{2,3},{3,2},{4,5},{5,4},{6,7},{7,6},{8,9},{9,8},{10,11... | collective-permute-start | bytes 61448 | tf_op jit(solution)/shard_map/ppermute | solution.py:499
  42.5 1.0 %shard_map.70 = (f32[40,128]{1,0:T(8,128)S(1)}, f32[2,40,128]{2,1,0:T(8,128)}) custom-call(f32[40,128]{1,0:T(8,128)S(1)} %get-tuple-element.81.e_ref, f32[40,128]{1,0:T(8,128)S(1)} %get-tuple-element.82.s_ref, bf16[20,80,128]{2,1,0:T(8,128)(2,1)S(1)} %get-tuple-element.62.time_ref, f32[40,128]{1,0:T(8,128)S(1)} %get-tuple-element.83.refs_0_, ...), custom_call_target="tpu_custom_call" | custom-call | tf_op jit(solution)/shard_map/pallas_call | solution.py:473
  43.5 3.0 %collective-permute-done.8.refs_0_ = f32[40,128]{1,0:T(8,128)S(1)} collective-permute-done((f32[40,128]{1,0:T(8,128)S(1)}, f32[40,128]{1,0:T(8,128)S(1)}, u32[]{:S(2)}, u32[]{:S(2)}) %collective-permute-start.8) | collective-permute-done | bytes 20512 | tf_op jit(solution)/shard_map/ppermute | solution.py:496
  46.5 0.0 collective-permute-done.9.refs_1_
  46.5 1.0 %shard_map.71 = f32[2,40,128]{2,1,0:T(8,128)} custom-call(f32[40,128]{1,0:T(8,128)S(1)} %get-tuple-element.86.r_ref, f32[40,128]{1,0:T(8,128)S(1)} %collective-permute-done.8.refs_0_, f32[40,128]{1,0:T(8,128)S(1)} %collective-permute-done.9.refs_1_, bf16[4,20,80,128]{3,2,1,0:T(8,128)(2,1)S(1)} %get-tuple-element.55.m_ref.refs_5_.refs_2_, ...), custom_call_target="tpu_custom_call" | custom-call | tf_op jit(solution)/shard_map/pallas_call | solution.py:473
  (2 shorter events, 0.0 us)
Async XLA Ops:
  6.5 9.6 %collective-permute-start.1 = (f32[40,128]{1,0:T(8,128)S(1)}, f32[40,128]{1,0:T(8,128)S(1)}, u32[]{:S(2)}, u32[]{:S(2)}) collective-permute-start(f32[40,128]{1,0:T(8,128)S(1)} %get-tuple-element.64), channel_id=1, source_target_pairs={{0,1},{1,3},{2,0},{3,2},{4,5},{5,7},{6,4},{7,6},{8,9},{9,11},{10,8... | collective-permute-start | bytes 61448 | tf_op jit(solution)/shard_map/ppermute | solution.py:496
  7.2 8.9 %collective-permute-start.2 = (f32[40,128]{1,0:T(8,128)S(1)}, f32[40,128]{1,0:T(8,128)S(1)}, u32[]{:S(2)}, u32[]{:S(2)}) collective-permute-start(f32[40,128]{1,0:T(8,128)S(1)} %get-tuple-element.65), channel_id=1, source_target_pairs={{0,1},{1,0},{2,3},{3,2},{4,5},{5,4},{6,7},{7,6},{8,9},{9,8},{10,11... | collective-permute-start | bytes 61448 | tf_op jit(solution)/shard_map/ppermute | solution.py:499
  9.2 8.2 %collective-permute-start = (f32[40,128]{1,0:T(8,128)S(1)}, f32[40,128]{1,0:T(8,128)S(1)}, u32[]{:S(2)}, u32[]{:S(2)}) collective-permute-start(f32[40,128]{1,0:T(8,128)S(1)} %get-tuple-element.63), channel_id=1, source_target_pairs={{0,30},{3,5},{4,2},{7,9},{8,6},{11,13},{12,10},{15,17},{16,14},{19... | collective-permute-start | bytes 61448 | tf_op jit(solution)/shard_map/ppermute | solution.py:496
  20.1 2.1 %collective-permute-start.4 = (f32[40,128]{1,0:T(8,128)S(1)}, f32[40,128]{1,0:T(8,128)S(1)}, u32[]{:S(2)}, u32[]{:S(2)}) collective-permute-start(f32[40,128]{1,0:T(8,128)S(1)} %get-tuple-element.74), channel_id=1, source_target_pairs={{0,2},{1,0},{2,3},{3,1},{4,6},{5,4},{6,7},{7,5},{8,10},{9,8},{10,1... | collective-permute-start | bytes 61448 | tf_op jit(solution)/shard_map/ppermute | solution.py:496
  20.1 2.1 %collective-permute-start.5 = (f32[40,128]{1,0:T(8,128)S(1)}, f32[40,128]{1,0:T(8,128)S(1)}, u32[]{:S(2)}, u32[]{:S(2)}) collective-permute-start(f32[40,128]{1,0:T(8,128)S(1)} %get-tuple-element.75), channel_id=1, source_target_pairs={{0,1},{1,0},{2,3},{3,2},{4,5},{5,4},{6,7},{7,6},{8,9},{9,8},{10,11... | collective-permute-start | bytes 61448 | tf_op jit(solution)/shard_map/ppermute | solution.py:499
  20.6 9.3 %collective-permute-start.3 = (f32[40,128]{1,0:T(8,128)S(1)}, f32[40,128]{1,0:T(8,128)S(1)}, u32[]{:S(2)}, u32[]{:S(2)}) collective-permute-start(f32[40,128]{1,0:T(8,128)S(1)} %get-tuple-element.73), channel_id=1, source_target_pairs={{1,31},{2,4},{5,3},{6,8},{9,7},{10,12},{13,11},{14,16},{17,15},{18... | collective-permute-start | bytes 61448 | tf_op jit(solution)/shard_map/ppermute | solution.py:496
  32.5 3.8 %collective-permute-start.6 = (f32[40,128]{1,0:T(8,128)S(1)}, f32[40,128]{1,0:T(8,128)S(1)}, u32[]{:S(2)}, u32[]{:S(2)}) collective-permute-start(f32[40,128]{1,0:T(8,128)S(1)} %get-tuple-element.78), channel_id=1, source_target_pairs={{0,30},{1,3},{2,0},{3,5},{4,2},{5,7},{6,4},{7,9},{8,6},{9,11},{10,... | collective-permute-start | bytes 61448 | tf_op jit(solution)/shard_map/ppermute | solution.py:496
  32.5 3.8 %collective-permute-start.7 = (f32[40,128]{1,0:T(8,128)S(1)}, f32[40,128]{1,0:T(8,128)S(1)}, u32[]{:S(2)}, u32[]{:S(2)}) collective-permute-start(f32[40,128]{1,0:T(8,128)S(1)} %get-tuple-element.79), channel_id=1, source_target_pairs={{0,1},{1,0},{2,3},{3,2},{4,5},{5,4},{6,7},{7,6},{8,9},{9,8},{10,11... | collective-permute-start | bytes 61448 | tf_op jit(solution)/shard_map/ppermute | solution.py:499
  39.0 7.4 %collective-permute-start.8 = (f32[40,128]{1,0:T(8,128)S(1)}, f32[40,128]{1,0:T(8,128)S(1)}, u32[]{:S(2)}, u32[]{:S(2)}) collective-permute-start(f32[40,128]{1,0:T(8,128)S(1)} %get-tuple-element.87), channel_id=1, source_target_pairs={{0,2},{1,31},{2,4},{3,1},{4,6},{5,3},{6,8},{7,5},{8,10},{9,7},{10,... | collective-permute-start | bytes 61448 | tf_op jit(solution)/shard_map/ppermute | solution.py:496
  39.1 7.4 %collective-permute-start.9 = (f32[40,128]{1,0:T(8,128)S(1)}, f32[40,128]{1,0:T(8,128)S(1)}, u32[]{:S(2)}, u32[]{:S(2)}) collective-permute-start(f32[40,128]{1,0:T(8,128)S(1)} %get-tuple-element.88), channel_id=1, source_target_pairs={{0,1},{1,0},{2,3},{3,2},{4,5},{5,4},{6,7},{7,6},{8,9},{9,8},{10,11... | collective-permute-start | bytes 61448 | tf_op jit(solution)/shard_map/ppermute | solution.py:499

commit v3 on v2

--- a/solution.py
+++ b/solution.py
@@ -236,15 +236,15 @@
         s = s_ref[...]
         i_s = times_i(s)
         scale = total_of(q * q) + 1e-6
-        live = index.astype(F32) < steps
-        alpha_re = jnp.where(live, total_of(q * s) / scale, 0.0)
-        alpha_im = jnp.where(live, -total_of(q * i_s) / scale, 0.0)
+        alpha_re = total_of(q * s) / scale
+        alpha_im = -total_of(q * i_s) / scale
         e_ref[...] += scaled(alpha_re, s) + scaled(alpha_im, i_s)
         w_ref[...] += scaled(alpha_re, back_z) + scaled(alpha_im, times_i(back_z))
         s_ref[...] = s - (scaled(alpha_re, q) + scaled(alpha_im, times_i(q)))
         return carry
 
-    lax.fori_loop(0, MR_MAX if mine is None else jnp.where(mine, MR_MAX, 0), step, 0)
+    count = jnp.minimum(steps[0, 0], MR_MAX)
+    lax.fori_loop(0, count if mine is None else jnp.where(mine, count, 0), step, 0)
 
 
 def send(half, e, w_ref, mt_ref, mz_ref, time_ref, rows_ref, spread_ref, back_ref):
@@ -345,7 +345,7 @@
                 copies[-2].wait()
                 copies[-1].wait()
                 for k in range(2):
-                    steps_ref[k] = jnp.full(steps_ref.shape[1:], count_ref[0, 0, k].astype(F32))
+                    steps_ref[k] = jnp.full(steps_ref.shape[1:], count_ref[0, 0, k])
                 own_ref[...] = pack_field(rhs_ref, half)
                 other_ref[...] = pack_field(rhs_ref, 1 - half)
 
@@ -453,7 +453,7 @@
     vector = jax.ShapeDtypeStruct((dof, width), F32)
     matrix = jax.ShapeDtypeStruct((dof // 2, 2 * dof, width), BF16)
     matrices = jax.ShapeDtypeStruct((4,) + matrix.shape, BF16)
-    counts = jax.ShapeDtypeStruct((2, 8, width), F32)
+    counts = jax.ShapeDtypeStruct((2, 8, width), jnp.int32)
     pair = jax.ShapeDtypeStruct((2, dof, width), F32)
     field = pltpu.VMEM((dof, width), F32)
     ab = pltpu.VMEM((4, 2, 2, 2 * dof, width), BF16)

time: 47.7 us -> 47.4 us (level)
  starting transfers between devices: 14.8 us -> 13.8 us
    ppermute x6, starting transfers between devices: 8.77 us -> 7.65 us  [along_time(): return lax.ppermute(mt, ('ta', 'sa'), time_pairs(colour, late))]
where the time goes in v3:
time: 47.4 us; the launch traced here: 47.2 us
  Pallas kernels  16.8 us (35%)
  waiting for transfers between devices  15.8 us (33%)
  starting transfers between devices  13.8 us (29%)
  between operations  0.76 us (2%)
    pallas_call x13, Pallas kernels, call(): pl.pallas_call(kernel, in_specs=specs or [VMEM] * len(ins), out_specs=[VM...  16.8 us
    ppermute x6, waiting for transfers between devices, along_time(): return lax.ppermute(mt, ('ta', 'sa'), time_pairs(colour, late))  15.8 us
    ppermute x6, starting transfers between devices, along_time(): return lax.ppermute(mt, ('ta', 'sa'), time_pairs(colour, late))  7.65 us
    ppermute x4, starting transfers between devices, along_z(): got = [lax.ppermute(mz, 'sa', [(s, (s - 1) % n_s) for s in range(n_s)])]  6.2 us
  transfers between devices with their start and end apart: 10, of which 4 were waited for; matrix products, arithmetic and copies ran while one was open for 0% of the time, Pallas kernels for 4%

profile of v3, /device:TPU:0, one launch (start us, length us, event | category | flops | bytes accessed | tf_op | source)
XLA Modules:
  0.0 47.2 jit_solution(16019243881676885259)
XLA Ops:
  0.6 3.3 %shard_map.59 = (bf16[4,20,80,128]{3,2,1,0:T(8,128)(2,1)S(1)}, bf16[20,80,128]{2,1,0:T(8,128)(2,1)S(1)}, bf16[4,20,80,128]{3,2,1,0:T(8,128)(2,1)S(1)}, bf16[20,8...) custom-call(s32[1,1,2]{2,1,0:T(1,128)} %refs_0_.3, ...), custom_call_target="tpu_custom_call" | custom-call | tf_op jit(solution)/shard_map/pallas_call | solution.py:473
  3.9 2.5 %shard_map.61 = (f32[40,128]{1,0:T(8,128)S(1)}, f32[40,128]{1,0:T(8,128)S(1)}, f32[40,128]{1,0:T(8,128)S(1)}, f32[40,128]{1,0:T(8,128)S(1)}) custom-call(s32[2,8,128]{2,1,0:T(8,128)S(1)} %get-tuple-element.52.refs_10_.steps_ref, f32[40,128]{1,0:T(8,128)S(1)} %get-tuple-element.50.refs_8_.r_ref, bf16[4,20,80,128]{3,2,1,0:T(8,128)(2,1)S(1)} %get-tuple-element.46.refs_4_.m_ref, ...), custom_call_target="tpu_custom_call" | custom-call | tf_op jit(solution)/shard_map/pallas_call | solution.py:473
  6.4 0.1 shard_map.60
  6.5 0.1 shard_map.62
  6.6 0.0 collective-permute-start.1
  6.7 2.7 %collective-permute-start.2 = (f32[40,128]{1,0:T(8,128)S(1)}, f32[40,128]{1,0:T(8,128)S(1)}, u32[]{:S(2)}, u32[]{:S(2)}) collective-permute-start(f32[40,128]{1,0:T(8,128)S(1)} %get-tuple-element.65), channel_id=1, source_target_pairs={{0,1},{1,0},{2,3},{3,2},{4,5},{5,4},{6,7},{7,6},{8,9},{9,8},{10,11... | collective-permute-start | bytes 61448 | tf_op jit(solution)/shard_map/ppermute | solution.py:499
  9.3 6.2 %collective-permute-start = (f32[40,128]{1,0:T(8,128)S(1)}, f32[40,128]{1,0:T(8,128)S(1)}, u32[]{:S(2)}, u32[]{:S(2)}) collective-permute-start(f32[40,128]{1,0:T(8,128)S(1)} %get-tuple-element.63), channel_id=1, source_target_pairs={{0,30},{3,5},{4,2},{7,9},{8,6},{11,13},{12,10},{15,17},{16,14},{19... | collective-permute-start | bytes 61448 | tf_op jit(solution)/shard_map/ppermute | solution.py:496
  15.6 0.2 shard_map.63.refs_1_
  15.8 0.0 collective-permute-done.1.refs_3_
  15.8 0.0 collective-permute-done.2.refs_4_
  15.8 1.3 %collective-permute-done.refs_2_ = f32[40,128]{1,0:T(8,128)S(1)} collective-permute-done((f32[40,128]{1,0:T(8,128)S(1)}, f32[40,128]{1,0:T(8,128)S(1)}, u32[]{:S(2)}, u32[]{:S(2)}) %collective-permute-start) | collective-permute-done | bytes 20512 | tf_op jit(solution)/shard_map/ppermute | solution.py:496
  17.1 2.8 %shard_map.65 = (f32[40,128]{1,0:T(8,128)S(1)}, f32[40,128]{1,0:T(8,128)S(1)}, f32[40,128]{1,0:T(8,128)S(1)}, f32[40,128]{1,0:T(8,128)S(1)}, f32[40,128]{1,0:T(8,128)S(1)}) custom-call(s32[2,8,128]{2,1,0:T(8,128)S(1)} %get-tuple-element.53.steps_ref.refs_0_, ...), custom_call_target="tpu_custom_call", output_to_operand_aliasing={{0}: (7, {}), {1}: (8, {}), {2}: (9, {}), {3}: (10, {})} | custom-call | tf_op jit(solution)/shard_map/pallas_call | solution.py:473
  19.9 0.0 collective-permute-start.4
  19.9 0.5 %collective-permute-start.5 = (f32[40,128]{1,0:T(8,128)S(1)}, f32[40,128]{1,0:T(8,128)S(1)}, u32[]{:S(2)}, u32[]{:S(2)}) collective-permute-start(f32[40,128]{1,0:T(8,128)S(1)} %get-tuple-element.75), channel_id=1, source_target_pairs={{0,1},{1,0},{2,3},{3,2},{4,5},{5,4},{6,7},{7,6},{8,9},{9,8},{10,11... | collective-permute-start | bytes 61448 | tf_op jit(solution)/shard_map/ppermute | solution.py:499
  20.4 1.3 %collective-permute-start.3 = (f32[40,128]{1,0:T(8,128)S(1)}, f32[40,128]{1,0:T(8,128)S(1)}, u32[]{:S(2)}, u32[]{:S(2)}) collective-permute-start(f32[40,128]{1,0:T(8,128)S(1)} %get-tuple-element.73), channel_id=1, source_target_pairs={{1,31},{2,4},{5,3},{6,8},{9,7},{10,12},{13,11},{14,16},{17,15},{18... | collective-permute-start | bytes 61448 | tf_op jit(solution)/shard_map/ppermute | solution.py:496
  21.7 0.3 shard_map.66.refs_1_
  22.0 0.0 collective-permute-done.4.refs_3_
  22.0 0.0 collective-permute-done.5.refs_4_
  22.0 7.6 %collective-permute-done.3.refs_2_ = f32[40,128]{1,0:T(8,128)S(1)} collective-permute-done((f32[40,128]{1,0:T(8,128)S(1)}, f32[40,128]{1,0:T(8,128)S(1)}, u32[]{:S(2)}, u32[]{:S(2)}) %collective-permute-start.3) | collective-permute-done | bytes 20512 | tf_op jit(solution)/shard_map/ppermute | solution.py:496
  29.6 2.6 %shard_map.67 = (f32[40,128]{1,0:T(8,128)S(1)}, f32[40,128]{1,0:T(8,128)S(1)}, f32[40,128]{1,0:T(8,128)S(1)}, f32[40,128]{1,0:T(8,128)S(1)}, f32[40,128]{1,0:T(8,128)S(1)}) custom-call(s32[2,8,128]{2,1,0:T(8,128)S(1)} %get-tuple-element.53.steps_ref.refs_0_, f32[40,128]{1,0:T(8,128)S(1)} %shard_map.66.refs_1_, f32[40,128]{1,0:T(8,128)S(1)} %collective-permute-done.3.refs_2_, ...), custom_call_target="tpu_custom_call" | custom-call | tf_op jit(solution)/shard_map/pallas_call | solution.py:473
  32.2 0.1 collective-permute-start.6
  32.3 0.1 collective-permute-start.7
  32.4 0.2 shard_map.68.refs_1_
  32.6 3.5 %collective-permute-done.6.refs_2_ = f32[40,128]{1,0:T(8,128)S(1)} collective-permute-done((f32[40,128]{1,0:T(8,128)S(1)}, f32[40,128]{1,0:T(8,128)S(1)}, u32[]{:S(2)}, u32[]{:S(2)}) %collective-permute-start.6) | collective-permute-done | bytes 20512 | tf_op jit(solution)/shard_map/ppermute | solution.py:496
  36.0 0.0 collective-permute-done.7.refs_3_
  36.0 2.7 %shard_map.69 = (f32[40,128]{1,0:T(8,128)S(1)}, f32[40,128]{1,0:T(8,128)S(1)}, f32[40,128]{1,0:T(8,128)S(1)}, f32[40,128]{1,0:T(8,128)S(1)}, f32[40,128]{1,0:T(8,128)S(1)}) custom-call(s32[2,8,128]{2,1,0:T(8,128)S(1)} %get-tuple-element.53.steps_ref.refs_0_, f32[40,128]{1,0:T(8,128)S(1)} %shard_map.68.refs_1_, f32[40,128]{1,0:T(8,128)S(1)} %collective-permute-done.6.refs_2_, ...), custom_call_target="tpu_custom_call" | custom-call | tf_op jit(solution)/shard_map/pallas_call | solution.py:473
  38.8 0.0 collective-permute-start.8
  38.8 3.0 %collective-permute-start.9 = (f32[40,128]{1,0:T(8,128)S(1)}, f32[40,128]{1,0:T(8,128)S(1)}, u32[]{:S(2)}, u32[]{:S(2)}) collective-permute-start(f32[40,128]{1,0:T(8,128)S(1)} %get-tuple-element.88), channel_id=1, source_target_pairs={{0,1},{1,0},{2,3},{3,2},{4,5},{5,4},{6,7},{7,6},{8,9},{9,8},{10,11... | collective-permute-start | bytes 61448 | tf_op jit(solution)/shard_map/ppermute | solution.py:499
  41.8 1.0 %shard_map.70 = (f32[40,128]{1,0:T(8,128)S(1)}, f32[2,40,128]{2,1,0:T(8,128)}) custom-call(f32[40,128]{1,0:T(8,128)S(1)} %get-tuple-element.81.e_ref, f32[40,128]{1,0:T(8,128)S(1)} %get-tuple-element.82.s_ref, bf16[20,80,128]{2,1,0:T(8,128)(2,1)S(1)} %get-tuple-element.62.time_ref, f32[40,128]{1,0:T(8,128)S(1)} %get-tuple-element.83.refs_0_, ...), custom_call_target="tpu_custom_call" | custom-call | tf_op jit(solution)/shard_map/pallas_call | solution.py:473
  42.8 3.4 %collective-permute-done.8.refs_0_ = f32[40,128]{1,0:T(8,128)S(1)} collective-permute-done((f32[40,128]{1,0:T(8,128)S(1)}, f32[40,128]{1,0:T(8,128)S(1)}, u32[]{:S(2)}, u32[]{:S(2)}) %collective-permute-start.8) | collective-permute-done | bytes 20512 | tf_op jit(solution)/shard_map/ppermute | solution.py:496
  46.2 0.0 collective-permute-done.9.refs_1_
  46.2 1.0 %shard_map.71 = f32[2,40,128]{2,1,0:T(8,128)} custom-call(f32[40,128]{1,0:T(8,128)S(1)} %get-tuple-element.86.r_ref, f32[40,128]{1,0:T(8,128)S(1)} %collective-permute-done.8.refs_0_, f32[40,128]{1,0:T(8,128)S(1)} %collective-permute-done.9.refs_1_, bf16[4,20,80,128]{3,2,1,0:T(8,128)(2,1)S(1)} %get-tuple-element.55.m_ref.refs_5_.refs_2_, ...), custom_call_target="tpu_custom_call" | custom-call | tf_op jit(solution)/shard_map/pallas_call | solution.py:473
  (1 shorter events, 0.0 us)
Async XLA Ops:
  6.6 9.1 %collective-permute-start.1 = (f32[40,128]{1,0:T(8,128)S(1)}, f32[40,128]{1,0:T(8,128)S(1)}, u32[]{:S(2)}, u32[]{:S(2)}) collective-permute-start(f32[40,128]{1,0:T(8,128)S(1)} %get-tuple-element.64), channel_id=1, source_target_pairs={{0,1},{1,3},{2,0},{3,2},{4,5},{5,7},{6,4},{7,6},{8,9},{9,11},{10,8... | collective-permute-start | bytes 61448 | tf_op jit(solution)/shard_map/ppermute | solution.py:496
  6.7 9.1 %collective-permute-start.2 = (f32[40,128]{1,0:T(8,128)S(1)}, f32[40,128]{1,0:T(8,128)S(1)}, u32[]{:S(2)}, u32[]{:S(2)}) collective-permute-start(f32[40,128]{1,0:T(8,128)S(1)} %get-tuple-element.65), channel_id=1, source_target_pairs={{0,1},{1,0},{2,3},{3,2},{4,5},{5,4},{6,7},{7,6},{8,9},{9,8},{10,11... | collective-permute-start | bytes 61448 | tf_op jit(solution)/shard_map/ppermute | solution.py:499
  9.3 7.7 %collective-permute-start = (f32[40,128]{1,0:T(8,128)S(1)}, f32[40,128]{1,0:T(8,128)S(1)}, u32[]{:S(2)}, u32[]{:S(2)}) collective-permute-start(f32[40,128]{1,0:T(8,128)S(1)} %get-tuple-element.63), channel_id=1, source_target_pairs={{0,30},{3,5},{4,2},{7,9},{8,6},{11,13},{12,10},{15,17},{16,14},{19... | collective-permute-start | bytes 61448 | tf_op jit(solution)/shard_map/ppermute | solution.py:496
  19.9 2.1 %collective-permute-start.4 = (f32[40,128]{1,0:T(8,128)S(1)}, f32[40,128]{1,0:T(8,128)S(1)}, u32[]{:S(2)}, u32[]{:S(2)}) collective-permute-start(f32[40,128]{1,0:T(8,128)S(1)} %get-tuple-element.74), channel_id=1, source_target_pairs={{0,2},{1,0},{2,3},{3,1},{4,6},{5,4},{6,7},{7,5},{8,10},{9,8},{10,1... | collective-permute-start | bytes 61448 | tf_op jit(solution)/shard_map/ppermute | solution.py:496
  19.9 2.1 %collective-permute-start.5 = (f32[40,128]{1,0:T(8,128)S(1)}, f32[40,128]{1,0:T(8,128)S(1)}, u32[]{:S(2)}, u32[]{:S(2)}) collective-permute-start(f32[40,128]{1,0:T(8,128)S(1)} %get-tuple-element.75), channel_id=1, source_target_pairs={{0,1},{1,0},{2,3},{3,2},{4,5},{5,4},{6,7},{7,6},{8,9},{9,8},{10,11... | collective-permute-start | bytes 61448 | tf_op jit(solution)/shard_map/ppermute | solution.py:499
  20.4 9.3 %collective-permute-start.3 = (f32[40,128]{1,0:T(8,128)S(1)}, f32[40,128]{1,0:T(8,128)S(1)}, u32[]{:S(2)}, u32[]{:S(2)}) collective-permute-start(f32[40,128]{1,0:T(8,128)S(1)} %get-tuple-element.73), channel_id=1, source_target_pairs={{1,31},{2,4},{5,3},{6,8},{9,7},{10,12},{13,11},{14,16},{17,15},{18... | collective-permute-start | bytes 61448 | tf_op jit(solution)/shard_map/ppermute | solution.py:496
  32.2 3.8 %collective-permute-start.6 = (f32[40,128]{1,0:T(8,128)S(1)}, f32[40,128]{1,0:T(8,128)S(1)}, u32[]{:S(2)}, u32[]{:S(2)}) collective-permute-start(f32[40,128]{1,0:T(8,128)S(1)} %get-tuple-element.78), channel_id=1, source_target_pairs={{0,30},{1,3},{2,0},{3,5},{4,2},{5,7},{6,4},{7,9},{8,6},{9,11},{10,... | collective-permute-start | bytes 61448 | tf_op jit(solution)/shard_map/ppermute | solution.py:496
  32.3 3.8 %collective-permute-start.7 = (f32[40,128]{1,0:T(8,128)S(1)}, f32[40,128]{1,0:T(8,128)S(1)}, u32[]{:S(2)}, u32[]{:S(2)}) collective-permute-start(f32[40,128]{1,0:T(8,128)S(1)} %get-tuple-element.79), channel_id=1, source_target_pairs={{0,1},{1,0},{2,3},{3,2},{4,5},{5,4},{6,7},{7,6},{8,9},{9,8},{10,11... | collective-permute-start | bytes 61448 | tf_op jit(solution)/shard_map/ppermute | solution.py:499
  38.8 7.4 %collective-permute-start.8 = (f32[40,128]{1,0:T(8,128)S(1)}, f32[40,128]{1,0:T(8,128)S(1)}, u32[]{:S(2)}, u32[]{:S(2)}) collective-permute-start(f32[40,128]{1,0:T(8,128)S(1)} %get-tuple-element.87), channel_id=1, source_target_pairs={{0,2},{1,31},{2,4},{3,1},{4,6},{5,3},{6,8},{7,5},{8,10},{9,7},{10,... | collective-permute-start | bytes 61448 | tf_op jit(solution)/shard_map/ppermute | solution.py:496
  38.8 7.4 %collective-permute-start.9 = (f32[40,128]{1,0:T(8,128)S(1)}, f32[40,128]{1,0:T(8,128)S(1)}, u32[]{:S(2)}, u32[]{:S(2)}) collective-permute-start(f32[40,128]{1,0:T(8,128)S(1)} %get-tuple-element.88), channel_id=1, source_target_pairs={{0,1},{1,0},{2,3},{3,2},{4,5},{5,4},{6,7},{7,6},{8,9},{9,8},{10,11... | collective-permute-start | bytes 61448 | tf_op jit(solution)/shard_map/ppermute | solution.py:499
